TPU v7x, 32 devices: a whole 2x2x4 slice. The times are simulated.
32 devices in a mesh: groups: 2 (over x), tok: 16 (over z, y, core).
Axes of the slice: x: 2, y: 2, z: 4, core: 2. Of those that a mesh axis runs over, the one named last changes fastest.
Arguments:
- activations: bfloat16 [8, 4096, 128], P(None, ('groups', 'tok')), parts along dimension 1, may hold values from -1.796875 to 1.796875
- gradients: bfloat16 [8, 4096, 128], P(None, ('groups', 'tok')), parts along dimension 1, may hold values from -1.796875 to 1.796875
- queries: bfloat16 [64, 4096], P(None, ('groups', 'tok')), parts along dimension 1, may hold values from -0.125 to 0.125
- layer_ids: int32 [3], replicated, may hold values from 0 to 7
Outputs:
- influence: float32 [64, 4096], P(None, ('groups', 'tok')), parts along dimension 1
There are 2 independent parts, one for each index of `groups`. A program takes and returns all parts, laid end to end along the dimension named above; an argument that names none is the same for every part. Nothing has to cross between parts.
Inputs may be any that keep to these rules, and one draw needn't show every extreme that they name: `layer_ids`: indices of stored layers; they may repeat.
All inputs are finite; a program needn't handle non-finite values.
Results may differ from a plain program's by a relative error of at most 0.0029.
Values may be sent and summed in bfloat16 or wider, within the bound.
No kernel may reach another device: no remote copies, remote signals or barrier semaphores. Data moves between devices by JAX's collectives and lax.ppermute only.
A program may use at most 64 MiB of HBM per device.

v0:
```python
import jax
import jax.numpy as jnp
from jax import lax
from jax.sharding import PartitionSpec as P


def passed_along(block, axis, distance):
    devices = range(lax.axis_size(axis))
    route = [((i - distance) % len(devices), i) for i in devices]
    return lax.ppermute(block, axis, route)


def token_pair_function(local_token_block, passing_block):
    input_product_matrix = jnp.einsum(
        "qun,qpn->qup", local_token_block[0], passing_block[0], preferred_element_type=jnp.float32
    )
    grad_gram = jnp.einsum(
        "qun,qpn->qup", local_token_block[1], passing_block[1], preferred_element_type=jnp.float32
    )
    return jnp.sum(input_product_matrix * grad_gram, axis=0).astype(jnp.bfloat16)


def rows_term(kernel, visitor_queries):
    return lax.dot_general(
        visitor_queries, kernel, (((1,), (1,)), ((), ())), preferred_element_type=jnp.float32
    )


def body(activations, gradients, queries, layer_ids):
    local_token_block = jnp.stack(
        [jnp.take(activations, layer_ids, axis=0), jnp.take(gradients, layer_ids, axis=0)]
    )
    half_cycle = lax.axis_size("tok") // 2
    influence = rows_term(token_pair_function(local_token_block, local_token_block), queries)

    def upward(stream):
        return passed_along((stream[0], stream[1]), "tok", -1)

    def downward(stream):
        return passed_along((stream[0], stream[1]), "tok", 1)

    def turn(turn_index, carried_state):
        result, rising_block_payload, downward_data = carried_state
        rising_block_payload = upward(rising_block_payload)
        downward_data = downward(downward_data)
        result = result + rows_term(
            token_pair_function(local_token_block, rising_block_payload[0]), rising_block_payload[1]
        )
        result = result + rows_term(
            token_pair_function(local_token_block, downward_data[0]), downward_data[1]
        )
        return (result, rising_block_payload, downward_data)

    initial = (influence, (local_token_block, queries), (local_token_block, queries))
    influence, rising_block_payload, downward_data = lax.fori_loop(0, half_cycle - 1, turn, initial)
    rising_block_payload = upward(rising_block_payload)
    influence = influence + rows_term(
        token_pair_function(local_token_block, rising_block_payload[0]), rising_block_payload[1]
    )
    return influence


def solution(mesh):
    return jax.shard_map(
        body,
        mesh=mesh,
        in_specs=(
            P(None, ("groups", "tok"), None),
            P(None, ("groups", "tok"), None),
            P(None, ("groups", "tok")),
            P(),
        ),
        out_specs=P(None, ("groups", "tok")),
        check_vma=False,
    )
```

profile of v0, /device:TPU:0, one launch (start us, length us, event | category | flops | bytes accessed | tf_op | source)
XLA Modules:
  0.0 78.9 jit_solution(1737522119606937563)
XLA Ops:
  3.8 70.7 %while.18 = (s32[]{:T(128)}, f32[64,128]{1,0:T(8,128)S(1)}, bf16[2,3,128,128]{3,2,1,0:T(8,128)(2,1)S(1)}, bf16[64,128]{1,0:T(8,128)(2,1)S(1)}, bf16[2,3,128,128]...) while((s32[]{:T(128)}, f32[64,128]{1,0:T(8,128)S(1)}, ...), condition=%wide.region_4.0_spmd, body=%wide.region_1.5_spmd.sunk | while | flops 54706176 | bytes 4423933 | solution.py:55
  3.8 5.5 %collective-permute-start.3 = (bf16[2,3,128,128]{3,2,1,0:T(8,128)(2,1)S(1)}, bf16[2,3,128,128]{3,2,1,0:T(8,128)(2,1)S(1)}, u32[]{:S(2)}, u32[]{:S(2)}) collective-permute-start(bf16[2,3,128,128]{3,2,1,0:T(8,128)(2,1)S(1)} %get-tuple-element.131), channel_id=1, source_target_pairs={{1,0},{2,1},{3,2},{4,3},{5,4},{6,5},{7,6},{8,7},{9,8},{10,9},{11,1... | collective-permute-start | bytes 589832 | tf_op jit(solution)/shard_map/while/body/eval_jaxpr/ppermute | solution.py:10
  10.0 2.7 %collective-permute-done.2 = bf16[64,128]{1,0:T(8,128)(2,1)S(1)} collective-permute-done((bf16[64,128]{1,0:T(8,128)(2,1)S(1)}, bf16[64,128]{1,0:T(8,128)(2,1)S(1)}, u32[]{:S(2)}, u32[]{:S(2)}) %collective-permute-start.2) | collective-permute-done | bytes 16416 | tf_op jit(solution)/shard_map/while/body/eval_jaxpr/ppermute | solution.py:10
  12.7 3.2 %collective-permute-done = bf16[64,128]{1,0:T(8,128)(2,1)S(1)} collective-permute-done((bf16[64,128]{1,0:T(8,128)(2,1)S(1)}, bf16[64,128]{1,0:T(8,128)(2,1)S(1)}, u32[]{:S(2)}, u32[]{:S(2)}) %collective-permute-start) | collective-permute-done | bytes 16416 | tf_op jit(solution)/shard_map/while/body/eval_jaxpr/ppermute | solution.py:10
  16.1 1.9 %collective-permute-done.1 = bf16[2,3,128,128]{3,2,1,0:T(8,128)(2,1)S(1)} collective-permute-done((bf16[2,3,128,128]{3,2,1,0:T(8,128)(2,1)S(1)}, bf16[2,3,128,128]{3,2,1,0:T(8,128)(2,1)S(1)}, u32[]{:S(2)}, u32[]{:S(2)}) %collective-permute-start.1) | collective-permute-done | bytes 196640 | tf_op jit(solution)/shard_map/while/body/eval_jaxpr/ppermute | solution.py:10
  19.4 1.7 %collective-permute-start.1 = (bf16[2,3,128,128]{3,2,1,0:T(8,128)(2,1)S(1)}, bf16[2,3,128,128]{3,2,1,0:T(8,128)(2,1)S(1)}, u32[]{:S(2)}, u32[]{:S(2)}) collective-permute-start(bf16[2,3,128,128]{3,2,1,0:T(8,128)(2,1)S(1)} %get-tuple-element.133), channel_id=1, source_target_pairs={{15,0},{0,1},{1,2},{2,3},{3,4},{4,5},{5,6},{6,7},{7,8},{8,9},{9,10... | collective-permute-start | bytes 589832 | tf_op jit(solution)/shard_map/while/body/eval_jaxpr/ppermute | solution.py:10
  22.3 2.7 %collective-permute-done = bf16[64,128]{1,0:T(8,128)(2,1)S(1)} collective-permute-done((bf16[64,128]{1,0:T(8,128)(2,1)S(1)}, bf16[64,128]{1,0:T(8,128)(2,1)S(1)}, u32[]{:S(2)}, u32[]{:S(2)}) %collective-permute-start) | collective-permute-done | bytes 16416 | tf_op jit(solution)/shard_map/while/body/eval_jaxpr/ppermute | solution.py:10
  25.2 2.1 %collective-permute-done.1 = bf16[2,3,128,128]{3,2,1,0:T(8,128)(2,1)S(1)} collective-permute-done((bf16[2,3,128,128]{3,2,1,0:T(8,128)(2,1)S(1)}, bf16[2,3,128,128]{3,2,1,0:T(8,128)(2,1)S(1)}, u32[]{:S(2)}, u32[]{:S(2)}) %collective-permute-start.1) | collective-permute-done | bytes 196640 | tf_op jit(solution)/shard_map/while/body/eval_jaxpr/ppermute | solution.py:10
  28.7 1.7 %collective-permute-start.1 = (bf16[2,3,128,128]{3,2,1,0:T(8,128)(2,1)S(1)}, bf16[2,3,128,128]{3,2,1,0:T(8,128)(2,1)S(1)}, u32[]{:S(2)}, u32[]{:S(2)}) collective-permute-start(bf16[2,3,128,128]{3,2,1,0:T(8,128)(2,1)S(1)} %get-tuple-element.133), channel_id=1, source_target_pairs={{15,0},{0,1},{1,2},{2,3},{3,4},{4,5},{5,6},{6,7},{7,8},{8,9},{9,10... | collective-permute-start | bytes 589832 | tf_op jit(solution)/shard_map/while/body/eval_jaxpr/ppermute | solution.py:10
  31.5 2.6 %collective-permute-done = bf16[64,128]{1,0:T(8,128)(2,1)S(1)} collective-permute-done((bf16[64,128]{1,0:T(8,128)(2,1)S(1)}, bf16[64,128]{1,0:T(8,128)(2,1)S(1)}, u32[]{:S(2)}, u32[]{:S(2)}) %collective-permute-start) | collective-permute-done | bytes 16416 | tf_op jit(solution)/shard_map/while/body/eval_jaxpr/ppermute | solution.py:10
  34.3 2.2 %collective-permute-done.1 = bf16[2,3,128,128]{3,2,1,0:T(8,128)(2,1)S(1)} collective-permute-done((bf16[2,3,128,128]{3,2,1,0:T(8,128)(2,1)S(1)}, bf16[2,3,128,128]{3,2,1,0:T(8,128)(2,1)S(1)}, u32[]{:S(2)}, u32[]{:S(2)}) %collective-permute-start.1) | collective-permute-done | bytes 196640 | tf_op jit(solution)/shard_map/while/body/eval_jaxpr/ppermute | solution.py:10
  38.0 1.7 %collective-permute-start.1 = (bf16[2,3,128,128]{3,2,1,0:T(8,128)(2,1)S(1)}, bf16[2,3,128,128]{3,2,1,0:T(8,128)(2,1)S(1)}, u32[]{:S(2)}, u32[]{:S(2)}) collective-permute-start(bf16[2,3,128,128]{3,2,1,0:T(8,128)(2,1)S(1)} %get-tuple-element.133), channel_id=1, source_target_pairs={{15,0},{0,1},{1,2},{2,3},{3,4},{4,5},{5,6},{6,7},{7,8},{8,9},{9,10... | collective-permute-start | bytes 589832 | tf_op jit(solution)/shard_map/while/body/eval_jaxpr/ppermute | solution.py:10
  40.8 2.6 %collective-permute-done = bf16[64,128]{1,0:T(8,128)(2,1)S(1)} collective-permute-done((bf16[64,128]{1,0:T(8,128)(2,1)S(1)}, bf16[64,128]{1,0:T(8,128)(2,1)S(1)}, u32[]{:S(2)}, u32[]{:S(2)}) %collective-permute-start) | collective-permute-done | bytes 16416 | tf_op jit(solution)/shard_map/while/body/eval_jaxpr/ppermute | solution.py:10
  43.6 2.2 %collective-permute-done.1 = bf16[2,3,128,128]{3,2,1,0:T(8,128)(2,1)S(1)} collective-permute-done((bf16[2,3,128,128]{3,2,1,0:T(8,128)(2,1)S(1)}, bf16[2,3,128,128]{3,2,1,0:T(8,128)(2,1)S(1)}, u32[]{:S(2)}, u32[]{:S(2)}) %collective-permute-start.1) | collective-permute-done | bytes 196640 | tf_op jit(solution)/shard_map/while/body/eval_jaxpr/ppermute | solution.py:10
  47.2 1.7 %collective-permute-start.1 = (bf16[2,3,128,128]{3,2,1,0:T(8,128)(2,1)S(1)}, bf16[2,3,128,128]{3,2,1,0:T(8,128)(2,1)S(1)}, u32[]{:S(2)}, u32[]{:S(2)}) collective-permute-start(bf16[2,3,128,128]{3,2,1,0:T(8,128)(2,1)S(1)} %get-tuple-element.133), channel_id=1, source_target_pairs={{15,0},{0,1},{1,2},{2,3},{3,4},{4,5},{5,6},{6,7},{7,8},{8,9},{9,10... | collective-permute-start | bytes 589832 | tf_op jit(solution)/shard_map/while/body/eval_jaxpr/ppermute | solution.py:10
  50.1 2.6 %collective-permute-done = bf16[64,128]{1,0:T(8,128)(2,1)S(1)} collective-permute-done((bf16[64,128]{1,0:T(8,128)(2,1)S(1)}, bf16[64,128]{1,0:T(8,128)(2,1)S(1)}, u32[]{:S(2)}, u32[]{:S(2)}) %collective-permute-start) | collective-permute-done | bytes 16416 | tf_op jit(solution)/shard_map/while/body/eval_jaxpr/ppermute | solution.py:10
  52.9 2.2 %collective-permute-done.1 = bf16[2,3,128,128]{3,2,1,0:T(8,128)(2,1)S(1)} collective-permute-done((bf16[2,3,128,128]{3,2,1,0:T(8,128)(2,1)S(1)}, bf16[2,3,128,128]{3,2,1,0:T(8,128)(2,1)S(1)}, u32[]{:S(2)}, u32[]{:S(2)}) %collective-permute-start.1) | collective-permute-done | bytes 196640 | tf_op jit(solution)/shard_map/while/body/eval_jaxpr/ppermute | solution.py:10
  56.5 1.7 %collective-permute-start.1 = (bf16[2,3,128,128]{3,2,1,0:T(8,128)(2,1)S(1)}, bf16[2,3,128,128]{3,2,1,0:T(8,128)(2,1)S(1)}, u32[]{:S(2)}, u32[]{:S(2)}) collective-permute-start(bf16[2,3,128,128]{3,2,1,0:T(8,128)(2,1)S(1)} %get-tuple-element.133), channel_id=1, source_target_pairs={{15,0},{0,1},{1,2},{2,3},{3,4},{4,5},{5,6},{6,7},{7,8},{8,9},{9,10... | collective-permute-start | bytes 589832 | tf_op jit(solution)/shard_map/while/body/eval_jaxpr/ppermute | solution.py:10
  59.3 2.6 %collective-permute-done = bf16[64,128]{1,0:T(8,128)(2,1)S(1)} collective-permute-done((bf16[64,128]{1,0:T(8,128)(2,1)S(1)}, bf16[64,128]{1,0:T(8,128)(2,1)S(1)}, u32[]{:S(2)}, u32[]{:S(2)}) %collective-permute-start) | collective-permute-done | bytes 16416 | tf_op jit(solution)/shard_map/while/body/eval_jaxpr/ppermute | solution.py:10
  62.1 2.2 %collective-permute-done.1 = bf16[2,3,128,128]{3,2,1,0:T(8,128)(2,1)S(1)} collective-permute-done((bf16[2,3,128,128]{3,2,1,0:T(8,128)(2,1)S(1)}, bf16[2,3,128,128]{3,2,1,0:T(8,128)(2,1)S(1)}, u32[]{:S(2)}, u32[]{:S(2)}) %collective-permute-start.1) | collective-permute-done | bytes 196640 | tf_op jit(solution)/shard_map/while/body/eval_jaxpr/ppermute | solution.py:10
  65.7 1.7 %collective-permute-start.1 = (bf16[2,3,128,128]{3,2,1,0:T(8,128)(2,1)S(1)}, bf16[2,3,128,128]{3,2,1,0:T(8,128)(2,1)S(1)}, u32[]{:S(2)}, u32[]{:S(2)}) collective-permute-start(bf16[2,3,128,128]{3,2,1,0:T(8,128)(2,1)S(1)} %get-tuple-element.133), channel_id=1, source_target_pairs={{15,0},{0,1},{1,2},{2,3},{3,4},{4,5},{5,6},{6,7},{7,8},{8,9},{9,10... | collective-permute-start | bytes 589832 | tf_op jit(solution)/shard_map/while/body/eval_jaxpr/ppermute | solution.py:10
  68.6 2.6 %collective-permute-done = bf16[64,128]{1,0:T(8,128)(2,1)S(1)} collective-permute-done((bf16[64,128]{1,0:T(8,128)(2,1)S(1)}, bf16[64,128]{1,0:T(8,128)(2,1)S(1)}, u32[]{:S(2)}, u32[]{:S(2)}) %collective-permute-start) | collective-permute-done | bytes 16416 | tf_op jit(solution)/shard_map/while/body/eval_jaxpr/ppermute | solution.py:10
  71.4 2.2 %collective-permute-done.1 = bf16[2,3,128,128]{3,2,1,0:T(8,128)(2,1)S(1)} collective-permute-done((bf16[2,3,128,128]{3,2,1,0:T(8,128)(2,1)S(1)}, bf16[2,3,128,128]{3,2,1,0:T(8,128)(2,1)S(1)}, u32[]{:S(2)}, u32[]{:S(2)}) %collective-permute-start.1) | collective-permute-done | bytes 196640 | tf_op jit(solution)/shard_map/while/body/eval_jaxpr/ppermute | solution.py:10
  74.5 3.2 %collective-permute-done.5 = bf16[2,3,128,128]{3,2,1,0:T(8,128)(2,1)S(1)} collective-permute-done((bf16[2,3,128,128]{3,2,1,0:T(8,128)(2,1)S(1)}, bf16[2,3,128,128]{3,2,1,0:T(8,128)(2,1)S(1)}, u32[]{:S(2)}, u32[]{:S(2)}) %collective-permute-start.5) | collective-permute-done | bytes 196640 | tf_op jit(solution)/shard_map/ppermute | solution.py:10
  (127 shorter events, 23.3 us)
Async XLA Ops:
  3.8 12.1 %collective-permute-start.3 = (bf16[2,3,128,128]{3,2,1,0:T(8,128)(2,1)S(1)}, bf16[2,3,128,128]{3,2,1,0:T(8,128)(2,1)S(1)}, u32[]{:S(2)}, u32[]{:S(2)}) collective-permute-start(bf16[2,3,128,128]{3,2,1,0:T(8,128)(2,1)S(1)} %get-tuple-element.131), channel_id=1, source_target_pairs={{1,0},{2,1},{3,2},{4,3},{5,4},{6,5},{7,6},{8,7},{9,8},{10,9},{11,1... | collective-permute-start | bytes 589832 | tf_op jit(solution)/shard_map/while/body/eval_jaxpr/ppermute | solution.py:10
  10.0 5.9 %collective-permute-start = (bf16[64,128]{1,0:T(8,128)(2,1)S(1)}, bf16[64,128]{1,0:T(8,128)(2,1)S(1)}, u32[]{:S(2)}, u32[]{:S(2)}) collective-permute-start(bf16[64,128]{1,0:T(8,128)(2,1)S(1)} %get-tuple-element.134), channel_id=1, source_target_pairs={{15,0},{0,1},{1,2},{2,3},{3,4},{4,5},{5,6},{6,7},{7,8},{8,9},{9,10... | collective-permute-start | bytes 49160 | tf_op jit(solution)/shard_map/while/body/eval_jaxpr/ppermute | solution.py:10
  10.0 8.0 %collective-permute-start.1 = (bf16[2,3,128,128]{3,2,1,0:T(8,128)(2,1)S(1)}, bf16[2,3,128,128]{3,2,1,0:T(8,128)(2,1)S(1)}, u32[]{:S(2)}, u32[]{:S(2)}) collective-permute-start(bf16[2,3,128,128]{3,2,1,0:T(8,128)(2,1)S(1)} %get-tuple-element.133), channel_id=1, source_target_pairs={{15,0},{0,1},{1,2},{2,3},{3,4},{4,5},{5,6},{6,7},{7,8},{8,9},{9,10... | collective-permute-start | bytes 589832 | tf_op jit(solution)/shard_map/while/body/eval_jaxpr/ppermute | solution.py:10
  18.9 6.1 %collective-permute-start.3 = (bf16[2,3,128,128]{3,2,1,0:T(8,128)(2,1)S(1)}, bf16[2,3,128,128]{3,2,1,0:T(8,128)(2,1)S(1)}, u32[]{:S(2)}, u32[]{:S(2)}) collective-permute-start(bf16[2,3,128,128]{3,2,1,0:T(8,128)(2,1)S(1)} %get-tuple-element.131), channel_id=1, source_target_pairs={{1,0},{2,1},{3,2},{4,3},{5,4},{6,5},{7,6},{8,7},{9,8},{10,9},{11,1... | collective-permute-start | bytes 589832 | tf_op jit(solution)/shard_map/while/body/eval_jaxpr/ppermute | solution.py:10
  18.9 3.4 %collective-permute-start.2 = (bf16[64,128]{1,0:T(8,128)(2,1)S(1)}, bf16[64,128]{1,0:T(8,128)(2,1)S(1)}, u32[]{:S(2)}, u32[]{:S(2)}) collective-permute-start(bf16[64,128]{1,0:T(8,128)(2,1)S(1)} %get-tuple-element.132), channel_id=1, source_target_pairs={{1,0},{2,1},{3,2},{4,3},{5,4},{6,5},{7,6},{8,7},{9,8},{10,9},{11,1... | collective-permute-start | bytes 49160 | tf_op jit(solution)/shard_map/while/body/eval_jaxpr/ppermute | solution.py:10
  19.1 5.9 %collective-permute-start = (bf16[64,128]{1,0:T(8,128)(2,1)S(1)}, bf16[64,128]{1,0:T(8,128)(2,1)S(1)}, u32[]{:S(2)}, u32[]{:S(2)}) collective-permute-start(bf16[64,128]{1,0:T(8,128)(2,1)S(1)} %get-tuple-element.134), channel_id=1, source_target_pairs={{15,0},{0,1},{1,2},{2,3},{3,4},{4,5},{5,6},{6,7},{7,8},{8,9},{9,10... | collective-permute-start | bytes 49160 | tf_op jit(solution)/shard_map/while/body/eval_jaxpr/ppermute | solution.py:10
  19.4 7.8 %collective-permute-start.1 = (bf16[2,3,128,128]{3,2,1,0:T(8,128)(2,1)S(1)}, bf16[2,3,128,128]{3,2,1,0:T(8,128)(2,1)S(1)}, u32[]{:S(2)}, u32[]{:S(2)}) collective-permute-start(bf16[2,3,128,128]{3,2,1,0:T(8,128)(2,1)S(1)} %get-tuple-element.133), channel_id=1, source_target_pairs={{15,0},{0,1},{1,2},{2,3},{3,4},{4,5},{5,6},{6,7},{7,8},{8,9},{9,10... | collective-permute-start | bytes 589832 | tf_op jit(solution)/shard_map/while/body/eval_jaxpr/ppermute | solution.py:10
  28.2 6.0 %collective-permute-start.3 = (bf16[2,3,128,128]{3,2,1,0:T(8,128)(2,1)S(1)}, bf16[2,3,128,128]{3,2,1,0:T(8,128)(2,1)S(1)}, u32[]{:S(2)}, u32[]{:S(2)}) collective-permute-start(bf16[2,3,128,128]{3,2,1,0:T(8,128)(2,1)S(1)} %get-tuple-element.131), channel_id=1, source_target_pairs={{1,0},{2,1},{3,2},{4,3},{5,4},{6,5},{7,6},{8,7},{9,8},{10,9},{11,1... | collective-permute-start | bytes 589832 | tf_op jit(solution)/shard_map/while/body/eval_jaxpr/ppermute | solution.py:10
  28.2 3.4 %collective-permute-start.2 = (bf16[64,128]{1,0:T(8,128)(2,1)S(1)}, bf16[64,128]{1,0:T(8,128)(2,1)S(1)}, u32[]{:S(2)}, u32[]{:S(2)}) collective-permute-start(bf16[64,128]{1,0:T(8,128)(2,1)S(1)} %get-tuple-element.132), channel_id=1, source_target_pairs={{1,0},{2,1},{3,2},{4,3},{5,4},{6,5},{7,6},{8,7},{9,8},{10,9},{11,1... | collective-permute-start | bytes 49160 | tf_op jit(solution)/shard_map/while/body/eval_jaxpr/ppermute | solution.py:10
  28.2 5.9 %collective-permute-start = (bf16[64,128]{1,0:T(8,128)(2,1)S(1)}, bf16[64,128]{1,0:T(8,128)(2,1)S(1)}, u32[]{:S(2)}, u32[]{:S(2)}) collective-permute-start(bf16[64,128]{1,0:T(8,128)(2,1)S(1)} %get-tuple-element.134), channel_id=1, source_target_pairs={{15,0},{0,1},{1,2},{2,3},{3,4},{4,5},{5,6},{6,7},{7,8},{8,9},{9,10... | collective-permute-start | bytes 49160 | tf_op jit(solution)/shard_map/while/body/eval_jaxpr/ppermute | solution.py:10
  28.7 7.8 %collective-permute-start.1 = (bf16[2,3,128,128]{3,2,1,0:T(8,128)(2,1)S(1)}, bf16[2,3,128,128]{3,2,1,0:T(8,128)(2,1)S(1)}, u32[]{:S(2)}, u32[]{:S(2)}) collective-permute-start(bf16[2,3,128,128]{3,2,1,0:T(8,128)(2,1)S(1)} %get-tuple-element.133), channel_id=1, source_target_pairs={{15,0},{0,1},{1,2},{2,3},{3,4},{4,5},{5,6},{6,7},{7,8},{8,9},{9,10... | collective-permute-start | bytes 589832 | tf_op jit(solution)/shard_map/while/body/eval_jaxpr/ppermute | solution.py:10
  37.4 6.0 %collective-permute-start.3 = (bf16[2,3,128,128]{3,2,1,0:T(8,128)(2,1)S(1)}, bf16[2,3,128,128]{3,2,1,0:T(8,128)(2,1)S(1)}, u32[]{:S(2)}, u32[]{:S(2)}) collective-permute-start(bf16[2,3,128,128]{3,2,1,0:T(8,128)(2,1)S(1)} %get-tuple-element.131), channel_id=1, source_target_pairs={{1,0},{2,1},{3,2},{4,3},{5,4},{6,5},{7,6},{8,7},{9,8},{10,9},{11,1... | collective-permute-start | bytes 589832 | tf_op jit(solution)/shard_map/while/body/eval_jaxpr/ppermute | solution.py:10
  37.5 5.9 %collective-permute-start = (bf16[64,128]{1,0:T(8,128)(2,1)S(1)}, bf16[64,128]{1,0:T(8,128)(2,1)S(1)}, u32[]{:S(2)}, u32[]{:S(2)}) collective-permute-start(bf16[64,128]{1,0:T(8,128)(2,1)S(1)} %get-tuple-element.134), channel_id=1, source_target_pairs={{15,0},{0,1},{1,2},{2,3},{3,4},{4,5},{5,6},{6,7},{7,8},{8,9},{9,10... | collective-permute-start | bytes 49160 | tf_op jit(solution)/shard_map/while/body/eval_jaxpr/ppermute | solution.py:10
  38.0 7.8 %collective-permute-start.1 = (bf16[2,3,128,128]{3,2,1,0:T(8,128)(2,1)S(1)}, bf16[2,3,128,128]{3,2,1,0:T(8,128)(2,1)S(1)}, u32[]{:S(2)}, u32[]{:S(2)}) collective-permute-start(bf16[2,3,128,128]{3,2,1,0:T(8,128)(2,1)S(1)} %get-tuple-element.133), channel_id=1, source_target_pairs={{15,0},{0,1},{1,2},{2,3},{3,4},{4,5},{5,6},{6,7},{7,8},{8,9},{9,10... | collective-permute-start | bytes 589832 | tf_op jit(solution)/shard_map/while/body/eval_jaxpr/ppermute | solution.py:10
  46.7 6.0 %collective-permute-start.3 = (bf16[2,3,128,128]{3,2,1,0:T(8,128)(2,1)S(1)}, bf16[2,3,128,128]{3,2,1,0:T(8,128)(2,1)S(1)}, u32[]{:S(2)}, u32[]{:S(2)}) collective-permute-start(bf16[2,3,128,128]{3,2,1,0:T(8,128)(2,1)S(1)} %get-tuple-element.131), channel_id=1, source_target_pairs={{1,0},{2,1},{3,2},{4,3},{5,4},{6,5},{7,6},{8,7},{9,8},{10,9},{11,1... | collective-permute-start | bytes 589832 | tf_op jit(solution)/shard_map/while/body/eval_jaxpr/ppermute | solution.py:10
  46.7 5.9 %collective-permute-start = (bf16[64,128]{1,0:T(8,128)(2,1)S(1)}, bf16[64,128]{1,0:T(8,128)(2,1)S(1)}, u32[]{:S(2)}, u32[]{:S(2)}) collective-permute-start(bf16[64,128]{1,0:T(8,128)(2,1)S(1)} %get-tuple-element.134), channel_id=1, source_target_pairs={{15,0},{0,1},{1,2},{2,3},{3,4},{4,5},{5,6},{6,7},{7,8},{8,9},{9,10... | collective-permute-start | bytes 49160 | tf_op jit(solution)/shard_map/while/body/eval_jaxpr/ppermute | solution.py:10
  47.2 7.8 %collective-permute-start.1 = (bf16[2,3,128,128]{3,2,1,0:T(8,128)(2,1)S(1)}, bf16[2,3,128,128]{3,2,1,0:T(8,128)(2,1)S(1)}, u32[]{:S(2)}, u32[]{:S(2)}) collective-permute-start(bf16[2,3,128,128]{3,2,1,0:T(8,128)(2,1)S(1)} %get-tuple-element.133), channel_id=1, source_target_pairs={{15,0},{0,1},{1,2},{2,3},{3,4},{4,5},{5,6},{6,7},{7,8},{8,9},{9,10... | collective-permute-start | bytes 589832 | tf_op jit(solution)/shard_map/while/body/eval_jaxpr/ppermute | solution.py:10
  55.9 6.0 %collective-permute-start.3 = (bf16[2,3,128,128]{3,2,1,0:T(8,128)(2,1)S(1)}, bf16[2,3,128,128]{3,2,1,0:T(8,128)(2,1)S(1)}, u32[]{:S(2)}, u32[]{:S(2)}) collective-permute-start(bf16[2,3,128,128]{3,2,1,0:T(8,128)(2,1)S(1)} %get-tuple-element.131), channel_id=1, source_target_pairs={{1,0},{2,1},{3,2},{4,3},{5,4},{6,5},{7,6},{8,7},{9,8},{10,9},{11,1... | collective-permute-start | bytes 589832 | tf_op jit(solution)/shard_map/while/body/eval_jaxpr/ppermute | solution.py:10
  56.0 5.9 %collective-permute-start = (bf16[64,128]{1,0:T(8,128)(2,1)S(1)}, bf16[64,128]{1,0:T(8,128)(2,1)S(1)}, u32[]{:S(2)}, u32[]{:S(2)}) collective-permute-start(bf16[64,128]{1,0:T(8,128)(2,1)S(1)} %get-tuple-element.134), channel_id=1, source_target_pairs={{15,0},{0,1},{1,2},{2,3},{3,4},{4,5},{5,6},{6,7},{7,8},{8,9},{9,10... | collective-permute-start | bytes 49160 | tf_op jit(solution)/shard_map/while/body/eval_jaxpr/ppermute | solution.py:10
  56.5 7.8 %collective-permute-start.1 = (bf16[2,3,128,128]{3,2,1,0:T(8,128)(2,1)S(1)}, bf16[2,3,128,128]{3,2,1,0:T(8,128)(2,1)S(1)}, u32[]{:S(2)}, u32[]{:S(2)}) collective-permute-start(bf16[2,3,128,128]{3,2,1,0:T(8,128)(2,1)S(1)} %get-tuple-element.133), channel_id=1, source_target_pairs={{15,0},{0,1},{1,2},{2,3},{3,4},{4,5},{5,6},{6,7},{7,8},{8,9},{9,10... | collective-permute-start | bytes 589832 | tf_op jit(solution)/shard_map/while/body/eval_jaxpr/ppermute | solution.py:10
  65.2 6.0 %collective-permute-start.3 = (bf16[2,3,128,128]{3,2,1,0:T(8,128)(2,1)S(1)}, bf16[2,3,128,128]{3,2,1,0:T(8,128)(2,1)S(1)}, u32[]{:S(2)}, u32[]{:S(2)}) collective-permute-start(bf16[2,3,128,128]{3,2,1,0:T(8,128)(2,1)S(1)} %get-tuple-element.131), channel_id=1, source_target_pairs={{1,0},{2,1},{3,2},{4,3},{5,4},{6,5},{7,6},{8,7},{9,8},{10,9},{11,1... | collective-permute-start | bytes 589832 | tf_op jit(solution)/shard_map/while/body/eval_jaxpr/ppermute | solution.py:10
  65.2 5.9 %collective-permute-start = (bf16[64,128]{1,0:T(8,128)(2,1)S(1)}, bf16[64,128]{1,0:T(8,128)(2,1)S(1)}, u32[]{:S(2)}, u32[]{:S(2)}) collective-permute-start(bf16[64,128]{1,0:T(8,128)(2,1)S(1)} %get-tuple-element.134), channel_id=1, source_target_pairs={{15,0},{0,1},{1,2},{2,3},{3,4},{4,5},{5,6},{6,7},{7,8},{8,9},{9,10... | collective-permute-start | bytes 49160 | tf_op jit(solution)/shard_map/while/body/eval_jaxpr/ppermute | solution.py:10
  65.7 7.8 %collective-permute-start.1 = (bf16[2,3,128,128]{3,2,1,0:T(8,128)(2,1)S(1)}, bf16[2,3,128,128]{3,2,1,0:T(8,128)(2,1)S(1)}, u32[]{:S(2)}, u32[]{:S(2)}) collective-permute-start(bf16[2,3,128,128]{3,2,1,0:T(8,128)(2,1)S(1)} %get-tuple-element.133), channel_id=1, source_target_pairs={{15,0},{0,1},{1,2},{2,3},{3,4},{4,5},{5,6},{6,7},{7,8},{8,9},{9,10... | collective-permute-start | bytes 589832 | tf_op jit(solution)/shard_map/while/body/eval_jaxpr/ppermute | solution.py:10
  74.5 3.6 %collective-permute-start.4 = (bf16[64,128]{1,0:T(8,128)(2,1)S(1)}, bf16[64,128]{1,0:T(8,128)(2,1)S(1)}, u32[]{:S(2)}, u32[]{:S(2)}) collective-permute-start(bf16[64,128]{1,0:T(8,128)(2,1)S(1)} %get-tuple-element.51), channel_id=1, source_target_pairs={{1,0},{2,1},{3,2},{4,3},{5,4},{6,5},{7,6},{8,7},{9,8},{10,9},{11,1... | collective-permute-start | bytes 49160 | tf_op jit(solution)/shard_map/ppermute | solution.py:10
  (8 other events, 21.9 us)
where the time goes:
time: 79.1 us; the launch traced here: 78.9 us
  waiting for transfers between devices  46 us (58%)
  starting transfers between devices  19.9 us (25%)
  matrix products  9.13 us (12%)
  local copies, waits for them, and re-layouts  3.32 us (4%)
    ppermute x30, waiting for transfers between devices, passed_along(): return lax.ppermute(block, axis, route)  46 us
    ppermute x30, starting transfers between devices, passed_along(): return lax.ppermute(block, axis, route)  19.9 us
    dot_general x16, matrix products, token_pair_function(): jnp.einsum('qun,qpn->qup', local_token_block[0], passing_block[0], prefer...  3.36 us
    dot_general x16, matrix products, token_pair_function(): jnp.einsum('qun,qpn->qup', local_token_block[1], passing_block[1], prefer...  3.04 us
    dot_general x16, matrix products, rows_term(): lax.dot_general(visitor_queries, kernel, (((1,), (1,)), ((), ())), prefer...  2.73 us
  transfers between devices with their start and end apart: 30, of which 22 were waited for; matrix products, arithmetic and copies ran while one was open for 2% of the time, Pallas kernels for 0%

commit v1 on v0

v1 whole, which is shorter than its diff:
```python
import functools

import jax
import jax.numpy as jnp
from jax import lax
from jax.experimental import pallas as pl
from jax.experimental.pallas import tpu as pltpu
from jax.sharding import PartitionSpec as P

VMEM = pltpu.VMEM
NT = (((1,), (1,)), ((), ()))
NN = (((1,), (0,)), ((), ()))


def params(mib):
    return pltpu.CompilerParams(vmem_limit_bytes=mib * 2**20)


def pair_cost(layers, tokens, width, q, pairs):
    return pl.CostEstimate(
        flops=2 * pairs * tokens * tokens * (2 * layers * width + q),
        bytes_accessed=2 * pairs * (2 * layers * tokens + q) * width,
        transcendentals=0,
    )


def vmem_specs(count):
    return [pl.BlockSpec(memory_space=VMEM)] * count


def pack_kernel(ids_ref, acts_ref, grads_ref, queries_ref, out_ref):
    layers, tokens = ids_ref.shape[0], acts_ref.shape[1]
    for l in range(layers):
        i = ids_ref[l]
        out_ref[2 * l * tokens : (2 * l + 1) * tokens] = acts_ref[i]
        out_ref[(2 * l + 1) * tokens : (2 * l + 2) * tokens] = grads_ref[i]
    out_ref[2 * layers * tokens :] = queries_ref[...]


def pack(ids, acts, grads, queries):
    layers, tokens = ids.shape[0], acts.shape[1]
    rows = 2 * layers * tokens + queries.shape[0]
    return pl.pallas_call(
        pack_kernel,
        out_shape=jax.ShapeDtypeStruct((rows, acts.shape[2]), acts.dtype),
        in_specs=[pl.BlockSpec(memory_space=pltpu.SMEM)] + vmem_specs(3),
        out_specs=pl.BlockSpec(memory_space=VMEM),
        compiler_params=params(8),
        name="pack",
    )(ids, acts, grads, queries)


def pair_block(layers, tokens, left, right):
    total = None
    for l in range(layers):
        a = slice(2 * l * tokens, (2 * l + 1) * tokens)
        g = slice((2 * l + 1) * tokens, (2 * l + 2) * tokens)
        x = lax.dot_general(left[a], right[a], NT, preferred_element_type=jnp.float32)
        y = lax.dot_general(left[g], right[g], NT, preferred_element_type=jnp.float32)
        total = x * y if total is None else total + x * y
    return total.astype(jnp.bfloat16)


def near_kernel(layers, tokens, count, *refs):
    own, out = refs[0], refs[count]
    total = None
    for other in refs[:count]:
        k = pair_block(layers, tokens, other, own)
        q = other[2 * layers * tokens :]
        term = lax.dot_general(q, k, NN, preferred_element_type=jnp.float32)
        total = term if total is None else total + term
    out[...] = total


def near(layers, tokens, members):
    q = members[0].shape[0] - 2 * layers * tokens
    return pl.pallas_call(
        functools.partial(near_kernel, layers, tokens, len(members)),
        out_shape=jax.ShapeDtypeStruct((q, tokens), jnp.float32),
        in_specs=vmem_specs(len(members)),
        out_specs=pl.BlockSpec(memory_space=VMEM),
        compiler_params=params(8),
        cost_estimate=pair_cost(layers, tokens, members[0].shape[1], q, len(members)),
        name="near",
    )(*members)


def far_kernel(layers, tokens, count, first, *refs):
    members, visitor = refs[:count], refs[count]
    before = None if first else refs[count + 1 : 2 * count + 1]
    back, parts = refs[-count - 1], refs[-count:]
    visitor_q = visitor[2 * layers * tokens :]
    total = None
    for j in range(count):
        k = pair_block(layers, tokens, members[j], visitor)
        q = members[j][2 * layers * tokens :]
        term = lax.dot_general(q, k, NN, preferred_element_type=jnp.float32)
        total = term if total is None else total + term
        part = lax.dot_general(visitor_q, k, NT, preferred_element_type=jnp.float32)
        parts[j][...] = part if first else before[j][...] + part
    back[...] = total


def far(layers, tokens, members, visitor, before):
    count, q = len(members), visitor.shape[0] - 2 * layers * tokens
    operands = [*members, visitor, *(before or [])]
    outs = pl.pallas_call(
        functools.partial(far_kernel, layers, tokens, count, before is None),
        out_shape=[jax.ShapeDtypeStruct((q, tokens), jnp.float32)] * (count + 1),
        in_specs=vmem_specs(len(operands)),
        out_specs=vmem_specs(count + 1),
        compiler_params=params(8),
        cost_estimate=pair_cost(layers, tokens, visitor.shape[1], 2 * q, count),
        name="far",
    )(*operands)
    return outs[0], list(outs[1:])


def body(acts, grads, queries, ids):
    n = lax.axis_size("tok")
    lanes = next(j for j in (4, 2, 1) if n % j == 0)
    planes = n // lanes
    layers, tokens = ids.shape[0], acts.shape[1]

    def across(x, lane):
        return lax.ppermute(x, "tok", [(i, i ^ lane) for i in range(n)])

    def plane_pairs(shift):
        if 2 * shift < planes:
            return [((p + shift) % planes, p) for p in range(planes)]
        half = [(p, p + shift) for p in range(shift)]
        return [(a, b) if a % 2 == 0 else (b, a) for a, b in half]

    def along(x, pairs):
        route = [(a * lanes + j, b * lanes + j) for a, b in pairs for j in range(lanes)]
        return lax.ppermute(x, "tok", route)

    mine = pack(ids, acts, grads, queries)
    routes = [plane_pairs(s) for s in range(planes // 2, 0, -1)]
    visitors = [along(mine, routes[0])] if routes else []
    members = [mine]
    if lanes > 2:
        members.append(across(mine, 2))
    visitors += [along(mine, r) for r in routes[1:]]
    if lanes > 1:
        members += [across(m, 1) for m in list(members)]
    order = [0, 2, 1, 3][: len(members)] if lanes > 2 else list(range(lanes))

    total = near(layers, tokens, members)
    parts, returned = None, []
    for visitor, route in zip(visitors, routes):
        back, parts = far(layers, tokens, members, visitor, parts)
        returned.append(along(back, [(b, a) for a, b in route]))
    if parts is not None:
        total = total + parts[0]
        for lane, part in list(zip(order, parts))[1:]:
            returned.append(across(part, lane))
    for r in returned:
        total = total + r
    return total


def solution(mesh):
    return jax.shard_map(
        body,
        mesh=mesh,
        in_specs=(
            P(None, ("groups", "tok"), None),
            P(None, ("groups", "tok"), None),
            P(None, ("groups", "tok")),
            P(),
        ),
        out_specs=P(None, ("groups", "tok")),
        check_vma=False,
    )
```

time: 79.1 us -> 34.5 us (0.44)
  waiting for transfers between devices: 46 us -> 9.08 us
  matrix products: 9.13 us -> 0 us
  Pallas kernels: 0 us -> 4.02 us
  starting transfers between devices: 19.9 us -> 17.2 us
    ppermute x30 -> x10, waiting for transfers between devices: 46 us -> 9.08 us  [the longest x4 8.31 us: along(): return lax.ppermute(x, 'tok', route)]
    dot_general x48 -> x0, matrix products: 9.13 us -> none  [the longest x16 3.36 us: token_pair_function(): jnp.einsum('qun,qpn->qup', local_token_block[0], passing_block[0], prefer...]
    pallas_call x0 -> x4, Pallas kernels: none -> 4.02 us  [the longest x2 2.47 us: far(): pl.pallas_call(functools.partial(far_kernel, layers, tokens, count, befor...]
    ppermute x30 -> x10, starting transfers between devices: 19.9 us -> 17.2 us  [the longest x4 12 us: along(): return lax.ppermute(x, 'tok', route)]
    unnamed x7 -> x8, local copies, waits for them, and re-layouts: 0.97 us -> 3.27 us
    gather x2 -> x0, local copies, waits for them, and re-layouts: 2.08 us -> none  [the longest x1 1.52 us: body(): jnp.take(gradients, layer_ids, axis=0)]
  transfers between devices with their start and end apart: 30 -> 10, of which waited for: 22 -> 4; matrix products, arithmetic and copies ran while one was open for 2% -> 0% of each run, Pallas kernels for 0% -> 6%
where the time goes in v1:
time: 34.5 us; the launch traced here: 34.3 us
  starting transfers between devices  17.2 us (50%)
  waiting for transfers between devices  9.08 us (26%)
  Pallas kernels  4.02 us (12%)
  local copies, waits for them, and re-layouts  3.27 us (9%)
  other arithmetic  0.63 us (2%)
    ppermute x4, starting transfers between devices, along(): return lax.ppermute(x, 'tok', route)  12 us
    ppermute x4, waiting for transfers between devices, along(): return lax.ppermute(x, 'tok', route)  8.31 us
    ppermute x6, starting transfers between devices, across(): return lax.ppermute(x, 'tok', [(i, i ^ lane) for i in range(n)])  5.21 us
    unnamed x8, local copies, waits for them, and re-layouts  3.27 us
    pallas_call x2, Pallas kernels, far(): pl.pallas_call(functools.partial(far_kernel, layers, tokens, count, befor...  2.47 us
    pallas_call x1, Pallas kernels, near(): pl.pallas_call(functools.partial(near_kernel, layers, tokens, len(members...  1 us
    ppermute x6, waiting for transfers between devices, across(): return lax.ppermute(x, 'tok', [(i, i ^ lane) for i in range(n)])  0.76 us
  transfers between devices with their start and end apart: 10, of which 4 were waited for; matrix products, arithmetic and copies ran while one was open for 0% of the time, Pallas kernels for 6%

profile of v1, /device:TPU:0, one launch (start us, length us, event | category | flops | bytes accessed | tf_op | source)
XLA Modules:
  0.0 34.3 jit_solution(17433499378097632688)
XLA Ops:
  0.0 0.9 %copy-done = bf16[8,128,128]{2,1,0:T(8,128)(2,1)S(1)} copy-done((bf16[8,128,128]{2,1,0:T(8,128)(2,1)S(1)}, bf16[8,128,128]{2,1,0:T(8,128)(2,1)}, u32[]{:S(2)}) %copy-start) | copy-done | bytes 262168
  1.0 0.9 %copy-done.1 = bf16[8,128,128]{2,1,0:T(8,128)(2,1)S(1)} copy-done((bf16[8,128,128]{2,1,0:T(8,128)(2,1)S(1)}, bf16[8,128,128]{2,1,0:T(8,128)(2,1)}, u32[]{:S(2)}) %copy-start.1) | copy-done | bytes 262168
  1.9 0.7 %copy-done.2 = bf16[64,128]{1,0:T(8,128)(2,1)S(1)} copy-done((bf16[64,128]{1,0:T(8,128)(2,1)S(1)}, bf16[64,128]{1,0:T(8,128)(2,1)}, u32[]{:S(2)}) %copy-start.2) | copy-done | bytes 16408
  2.6 0.7 %copy-done.3 = s32[3]{0:T(128)S(1)} copy-done((s32[3]{0:T(128)S(1)}, s32[3]{0:T(128)}, u32[]{:S(2)}) %copy-start.3) | copy-done | bytes 36
  3.3 0.6 %pack.1.refs_0_ = bf16[832,128]{1,0:T(8,128)(2,1)S(1)} custom-call(s32[3]{0:T(128)S(1)} %copy-done.3, bf16[8,128,128]{2,1,0:T(8,128)(2,1)S(1)} %copy-done, bf16[8,128,128]{2,1,0:T(8,128)(2,1)S(1)} %copy-done.1, bf16[64,128]{1,0:T(8,128)(2,1)S(1)} %copy-done.2), custom_call_target="tpu_custom_call" | custom-call | tf_op jit(solution)/shard_map/pack/pallas_call | solution.py:43
  3.8 3.1 %collective-permute-start = (bf16[832,128]{1,0:T(8,128)(2,1)S(1)}, bf16[832,128]{1,0:T(8,128)(2,1)S(1)}, u32[]{:S(2)}, u32[]{:S(2)}) collective-permute-start(bf16[832,128]{1,0:T(8,128)(2,1)S(1)} %pack.1.refs_0_), channel_id=1, source_target_pairs={{0,2},{1,3},{2,0},{3,1},{4,6},{5,7},{6,4},{7,5},{8,10},{9,11},{10,... | collective-permute-start | bytes 638984 | tf_op jit(solution)/shard_map/ppermute | solution.py:126
  6.9 0.0 collective-permute-start.1
  6.9 4.5 %collective-permute-start.4 = (bf16[832,128]{1,0:T(8,128)(2,1)S(1)}, bf16[832,128]{1,0:T(8,128)(2,1)S(1)}, u32[]{:S(2)}, u32[]{:S(2)}) collective-permute-start(bf16[832,128]{1,0:T(8,128)(2,1)S(1)} %pack.1.refs_0_), channel_id=1, source_target_pairs={{0,8},{1,9},{2,10},{3,11},{12,4},{13,5},{14,6},{15,7},{16,24},{17,... | collective-permute-start | bytes 638984 | tf_op jit(solution)/shard_map/ppermute | solution.py:136
  11.4 0.7 %collective-permute-done.refs_1_ = bf16[832,128]{1,0:T(8,128)(2,1)S(1)} collective-permute-done((bf16[832,128]{1,0:T(8,128)(2,1)S(1)}, bf16[832,128]{1,0:T(8,128)(2,1)S(1)}, u32[]{:S(2)}, u32[]{:S(2)}) %collective-permute-start) | collective-permute-done | bytes 213024 | tf_op jit(solution)/shard_map/ppermute | solution.py:126
  12.2 3.8 %collective-permute-start.3 = (bf16[832,128]{1,0:T(8,128)(2,1)S(1)}, bf16[832,128]{1,0:T(8,128)(2,1)S(1)}, u32[]{:S(2)}, u32[]{:S(2)}) collective-permute-start(bf16[832,128]{1,0:T(8,128)(2,1)S(1)} %pack.1.refs_0_), channel_id=1, source_target_pairs={{4,0},{5,1},{6,2},{7,3},{8,4},{9,5},{10,6},{11,7},{12,8},{13,9},{1... | collective-permute-start | bytes 638984 | tf_op jit(solution)/shard_map/ppermute | solution.py:136
  16.0 0.6 %collective-permute-done.4.refs_4_ = bf16[832,128]{1,0:T(8,128)(2,1)S(1)} collective-permute-done((bf16[832,128]{1,0:T(8,128)(2,1)S(1)}, bf16[832,128]{1,0:T(8,128)(2,1)S(1)}, u32[]{:S(2)}, u32[]{:S(2)}) %collective-permute-start.4) | collective-permute-done | bytes 213024 | tf_op jit(solution)/shard_map/ppermute | solution.py:136
  16.6 0.0 collective-permute-done.2.refs_3_
  16.6 1.2 %far.2 = (f32[64,128]{1,0:T(8,128)S(1)}, f32[64,128]{1,0:T(8,128)S(1)}, f32[64,128]{1,0:T(8,128)S(1)}, f32[64,128]{1,0:T(8,128)S(1)}, f32[64,128]{1,0:T(8,128)S(1)}) custom-call(bf16[832,128]{1,0:T(8,128)(2,1)S(1)} %pack.1.refs_0_, bf16[832,128]{1,0:T(8,128)(2,1)S(1)} %collective-permute-done.refs_1_, bf16[832,128]{1,0:T(8,128)(2,1)S(1)} %collective-permute-done.1.refs_2_, ...), custom_call_target="tpu_custom_call" | custom-call | flops 117440512 | bytes 917504 | tf_op jit(solution)/shard_map/far/pallas_call | solution.py:107
  17.8 3.4 %collective-permute-done.3.refs_4_ = bf16[832,128]{1,0:T(8,128)(2,1)S(1)} collective-permute-done((bf16[832,128]{1,0:T(8,128)(2,1)S(1)}, bf16[832,128]{1,0:T(8,128)(2,1)S(1)}, u32[]{:S(2)}, u32[]{:S(2)}) %collective-permute-start.3) | collective-permute-done | bytes 213024 | tf_op jit(solution)/shard_map/ppermute | solution.py:136
  21.2 1.2 %far.3 = (f32[64,128]{1,0:T(8,128)S(1)}, f32[64,128]{1,0:T(8,128)S(1)}, f32[64,128]{1,0:T(8,128)S(1)}, f32[64,128]{1,0:T(8,128)S(1)}, f32[64,128]{1,0:T(8,128)S(1)}) custom-call(bf16[832,128]{1,0:T(8,128)(2,1)S(1)} %pack.1.refs_0_, bf16[832,128]{1,0:T(8,128)(2,1)S(1)} %collective-permute-done.refs_1_, bf16[832,128]{1,0:T(8,128)(2,1)S(1)} %collective-permute-done.1.refs_2_, ...), custom_call_target="tpu_custom_call" | custom-call | flops 117440512 | bytes 917504 | tf_op jit(solution)/shard_map/far/pallas_call | solution.py:107
  22.4 2.4 %collective-permute-start.6 = (f32[64,128]{1,0:T(8,128)S(1)}, f32[64,128]{1,0:T(8,128)S(1)}, u32[]{:S(2)}, u32[]{:S(2)}) collective-permute-start(f32[64,128]{1,0:T(8,128)S(1)} %get-tuple-element.21), channel_id=1, source_target_pairs={{0,4},{1,5},{2,6},{3,7},{4,8},{5,9},{6,10},{7,11},{8,12},{9,13},{1... | collective-permute-start | bytes 98312 | tf_op jit(solution)/shard_map/ppermute | solution.py:136
  24.8 0.5 %collective-permute-start.7 = (f32[64,128]{1,0:T(8,128)S(1)}, f32[64,128]{1,0:T(8,128)S(1)}, u32[]{:S(2)}, u32[]{:S(2)}) collective-permute-start(f32[64,128]{1,0:T(8,128)S(1)} %get-tuple-element.22), channel_id=1, source_target_pairs={{0,2},{1,3},{2,0},{3,1},{4,6},{5,7},{6,4},{7,5},{8,10},{9,11},{10,... | collective-permute-start | bytes 98312 | tf_op jit(solution)/shard_map/ppermute | solution.py:126
  25.3 1.6 %collective-permute-start.9 = (f32[64,128]{1,0:T(8,128)S(1)}, f32[64,128]{1,0:T(8,128)S(1)}, u32[]{:S(2)}, u32[]{:S(2)}) collective-permute-start(f32[64,128]{1,0:T(8,128)S(1)} %get-tuple-element.24), channel_id=1, source_target_pairs={{0,3},{1,2},{2,1},{3,0},{4,7},{5,6},{6,5},{7,4},{8,11},{9,10},{10,... | collective-permute-start | bytes 98312 | tf_op jit(solution)/shard_map/ppermute | solution.py:126
  26.9 1.3 %collective-permute-start.5 = (f32[64,128]{1,0:T(8,128)S(1)}, f32[64,128]{1,0:T(8,128)S(1)}, u32[]{:S(2)}, u32[]{:S(2)}) collective-permute-start(f32[64,128]{1,0:T(8,128)S(1)} %get-tuple-element.20), channel_id=1, source_target_pairs={{8,0},{9,1},{10,2},{11,3},{4,12},{5,13},{6,14},{7,15},{24,16},{25,... | collective-permute-start | bytes 98312 | tf_op jit(solution)/shard_map/ppermute | solution.py:136
  28.2 1.0 %near.1 = f32[64,128]{1,0:T(8,128)S(1)} custom-call(bf16[832,128]{1,0:T(8,128)(2,1)S(1)} %pack.1.refs_0_, bf16[832,128]{1,0:T(8,128)(2,1)S(1)} %collective-permute-done.refs_1_, bf16[832,128]{1,0:T(8,128)(2,1)S(1)} %collective-permute-done.1.refs_2_, bf16[832,128]{1,0:T(8,128)(2,1)S(1)} %collective-permute-done.2.refs_3_), custom_call_target="tpu_custom_call" | custom-call | flops 109051904 | bytes 851968 | tf_op jit(solution)/shard_map/near/pallas_call | solution.py:77
  29.2 0.0 collective-permute-done.7
  29.2 0.0 collective-permute-done.8
  29.3 4.4 %collective-permute-done.5 = f32[64,128]{1,0:T(8,128)S(1)} collective-permute-done((f32[64,128]{1,0:T(8,128)S(1)}, f32[64,128]{1,0:T(8,128)S(1)}, u32[]{:S(2)}, u32[]{:S(2)}) %collective-permute-start.5) | collective-permute-done | bytes 32800 | tf_op jit(solution)/shard_map/ppermute | solution.py:136
  33.6 0.6 %add_add_fusion = f32[64,128]{1,0:T(8,128)} fusion(f32[64,128]{1,0:T(8,128)S(1)} %collective-permute-done.9, f32[64,128]{1,0:T(8,128)S(1)} %collective-permute-done.8, f32[64,128]{1,0:T(8,128)S(1)} %collective-permute-done.7, f32[64,128]{1,0:T(8,128)S(1)} %collective-permute-done.6, f32[64,128]{1,0:T(8,128)S(1)} %collective-permute-done.5, ...), kind=kLoop, calls=%fused_computation | loop fusion | flops 49152 | bytes 262144 | tf_op jit(solution)/shard_map/add | solution.py:159
  (9 shorter events, 0.0 us)
Async XLA Ops:
  0.0 0.9 %copy-start = (bf16[8,128,128]{2,1,0:T(8,128)(2,1)S(1)}, bf16[8,128,128]{2,1,0:T(8,128)(2,1)}, u32[]{:S(2)}) copy-start(bf16[8,128,128]{2,1,0:T(8,128)(2,1)} %acts_ref.1) | copy-start | bytes 786436
  1.0 0.9 %copy-start.1 = (bf16[8,128,128]{2,1,0:T(8,128)(2,1)S(1)}, bf16[8,128,128]{2,1,0:T(8,128)(2,1)}, u32[]{:S(2)}) copy-start(bf16[8,128,128]{2,1,0:T(8,128)(2,1)} %grads_ref.1) | copy-start | bytes 786436
  1.9 0.7 %copy-start.2 = (bf16[64,128]{1,0:T(8,128)(2,1)S(1)}, bf16[64,128]{1,0:T(8,128)(2,1)}, u32[]{:S(2)}) copy-start(bf16[64,128]{1,0:T(8,128)(2,1)} %queries_ref.1) | copy-start | bytes 49156
  2.6 0.7 %copy-start.3 = (s32[3]{0:T(128)S(1)}, s32[3]{0:T(128)}, u32[]{:S(2)}) copy-start(s32[3]{0:T(128)} %ids_ref.1) | copy-start | bytes 40
  3.8 8.3 %collective-permute-start = (bf16[832,128]{1,0:T(8,128)(2,1)S(1)}, bf16[832,128]{1,0:T(8,128)(2,1)S(1)}, u32[]{:S(2)}, u32[]{:S(2)}) collective-permute-start(bf16[832,128]{1,0:T(8,128)(2,1)S(1)} %pack.1.refs_0_), channel_id=1, source_target_pairs={{0,2},{1,3},{2,0},{3,1},{4,6},{5,7},{6,4},{7,5},{8,10},{9,11},{10,... | collective-permute-start | bytes 638984 | tf_op jit(solution)/shard_map/ppermute | solution.py:126
  6.9 9.1 %collective-permute-start.1 = (bf16[832,128]{1,0:T(8,128)(2,1)S(1)}, bf16[832,128]{1,0:T(8,128)(2,1)S(1)}, u32[]{:S(2)}, u32[]{:S(2)}) collective-permute-start(bf16[832,128]{1,0:T(8,128)(2,1)S(1)} %pack.1.refs_0_), channel_id=1, source_target_pairs={{0,1},{1,0},{2,3},{3,2},{4,5},{5,4},{6,7},{7,6},{8,9},{9,8},{10,11... | collective-permute-start | bytes 638984 | tf_op jit(solution)/shard_map/ppermute | solution.py:126
  6.9 9.7 %collective-permute-start.4 = (bf16[832,128]{1,0:T(8,128)(2,1)S(1)}, bf16[832,128]{1,0:T(8,128)(2,1)S(1)}, u32[]{:S(2)}, u32[]{:S(2)}) collective-permute-start(bf16[832,128]{1,0:T(8,128)(2,1)S(1)} %pack.1.refs_0_), channel_id=1, source_target_pairs={{0,8},{1,9},{2,10},{3,11},{12,4},{13,5},{14,6},{15,7},{16,24},{17,... | collective-permute-start | bytes 638984 | tf_op jit(solution)/shard_map/ppermute | solution.py:136
  12.2 4.4 %collective-permute-start.2 = (bf16[832,128]{1,0:T(8,128)(2,1)S(1)}, bf16[832,128]{1,0:T(8,128)(2,1)S(1)}, u32[]{:S(2)}, u32[]{:S(2)}) collective-permute-start(bf16[832,128]{1,0:T(8,128)(2,1)S(1)} %collective-permute-done.refs_1_), channel_id=1, source_target_pairs={{0,1},{1,0},{2,3},{3,2},{4,5},{5,4},{6,7},{7,6},{8,9},{9,8},{10,11... | collective-permute-start | bytes 638984 | tf_op jit(solution)/shard_map/ppermute | solution.py:126
  12.2 9.0 %collective-permute-start.3 = (bf16[832,128]{1,0:T(8,128)(2,1)S(1)}, bf16[832,128]{1,0:T(8,128)(2,1)S(1)}, u32[]{:S(2)}, u32[]{:S(2)}) collective-permute-start(bf16[832,128]{1,0:T(8,128)(2,1)S(1)} %pack.1.refs_0_), channel_id=1, source_target_pairs={{4,0},{5,1},{6,2},{7,3},{8,4},{9,5},{10,6},{11,7},{12,8},{13,9},{1... | collective-permute-start | bytes 638984 | tf_op jit(solution)/shard_map/ppermute | solution.py:136
  22.4 6.8 %collective-permute-start.6 = (f32[64,128]{1,0:T(8,128)S(1)}, f32[64,128]{1,0:T(8,128)S(1)}, u32[]{:S(2)}, u32[]{:S(2)}) collective-permute-start(f32[64,128]{1,0:T(8,128)S(1)} %get-tuple-element.21), channel_id=1, source_target_pairs={{0,4},{1,5},{2,6},{3,7},{4,8},{5,9},{6,10},{7,11},{8,12},{9,13},{1... | collective-permute-start | bytes 98312 | tf_op jit(solution)/shard_map/ppermute | solution.py:136
  24.8 4.4 %collective-permute-start.7 = (f32[64,128]{1,0:T(8,128)S(1)}, f32[64,128]{1,0:T(8,128)S(1)}, u32[]{:S(2)}, u32[]{:S(2)}) collective-permute-start(f32[64,128]{1,0:T(8,128)S(1)} %get-tuple-element.22), channel_id=1, source_target_pairs={{0,2},{1,3},{2,0},{3,1},{4,6},{5,7},{6,4},{7,5},{8,10},{9,11},{10,... | collective-permute-start | bytes 98312 | tf_op jit(solution)/shard_map/ppermute | solution.py:126
  25.3 3.9 %collective-permute-start.8 = (f32[64,128]{1,0:T(8,128)S(1)}, f32[64,128]{1,0:T(8,128)S(1)}, u32[]{:S(2)}, u32[]{:S(2)}) collective-permute-start(f32[64,128]{1,0:T(8,128)S(1)} %get-tuple-element.23), channel_id=1, source_target_pairs={{0,1},{1,0},{2,3},{3,2},{4,5},{5,4},{6,7},{7,6},{8,9},{9,8},{10,11... | collective-permute-start | bytes 98312 | tf_op jit(solution)/shard_map/ppermute | solution.py:126
  25.3 3.9 %collective-permute-start.9 = (f32[64,128]{1,0:T(8,128)S(1)}, f32[64,128]{1,0:T(8,128)S(1)}, u32[]{:S(2)}, u32[]{:S(2)}) collective-permute-start(f32[64,128]{1,0:T(8,128)S(1)} %get-tuple-element.24), channel_id=1, source_target_pairs={{0,3},{1,2},{2,1},{3,0},{4,7},{5,6},{6,5},{7,4},{8,11},{9,10},{10,... | collective-permute-start | bytes 98312 | tf_op jit(solution)/shard_map/ppermute | solution.py:126
  26.9 6.7 %collective-permute-start.5 = (f32[64,128]{1,0:T(8,128)S(1)}, f32[64,128]{1,0:T(8,128)S(1)}, u32[]{:S(2)}, u32[]{:S(2)}) collective-permute-start(f32[64,128]{1,0:T(8,128)S(1)} %get-tuple-element.20), channel_id=1, source_target_pairs={{8,0},{9,1},{10,2},{11,3},{4,12},{5,13},{6,14},{7,15},{24,16},{25,... | collective-permute-start | bytes 98312 | tf_op jit(solution)/shard_map/ppermute | solution.py:136

commit v2 on v1

v2 whole, which is shorter than its diff:
```python
import functools

import jax
import jax.numpy as jnp
from jax import lax
from jax.experimental import pallas as pl
from jax.experimental.pallas import tpu as pltpu
from jax.sharding import PartitionSpec as P

VMEM = pltpu.VMEM
NT = (((1,), (1,)), ((), ()))
NN = (((1,), (0,)), ((), ()))


def params(mib):
    return pltpu.CompilerParams(vmem_limit_bytes=mib * 2**20)


def pair_cost(layers, tokens, width, q, pairs):
    return pl.CostEstimate(
        flops=2 * pairs * tokens * tokens * (2 * layers * width + q),
        bytes_accessed=2 * pairs * (2 * layers * tokens + q) * width,
        transcendentals=0,
    )


def vmem_specs(count):
    return [pl.BlockSpec(memory_space=VMEM)] * count


def pack_kernel(ids_hbm, acts_hbm, grads_hbm, queries_hbm, out_ref, ids, acts, grads, sems):
    layers, tokens = ids.shape[0], acts.shape[1]
    queries = out_ref.at[pl.ds(2 * layers * tokens, queries_hbm.shape[0])]
    moves = [(ids_hbm, ids), (acts_hbm, acts), (grads_hbm, grads), (queries_hbm, queries)]
    copies = [pltpu.make_async_copy(*m, sems.at[i]) for i, m in enumerate(moves)]
    for c in copies:
        c.start()
    for c in copies:
        c.wait()
    for l in range(layers):
        i = ids[l]
        out_ref[2 * l * tokens : (2 * l + 1) * tokens] = acts[i]
        out_ref[(2 * l + 1) * tokens : (2 * l + 2) * tokens] = grads[i]


def pack(ids, acts, grads, queries):
    layers, tokens = ids.shape[0], acts.shape[1]
    rows = 2 * layers * tokens + queries.shape[0]
    held = [pltpu.with_memory_space_constraint(x, pltpu.HBM) for x in (ids, acts, grads, queries)]
    return pl.pallas_call(
        pack_kernel,
        out_shape=jax.ShapeDtypeStruct((rows, acts.shape[2]), acts.dtype),
        in_specs=[pl.BlockSpec(memory_space=pltpu.HBM)] * 4,
        out_specs=pl.BlockSpec(memory_space=VMEM),
        scratch_shapes=[
            pltpu.SMEM(ids.shape, ids.dtype),
            VMEM(acts.shape, acts.dtype),
            VMEM(grads.shape, grads.dtype),
            pltpu.SemaphoreType.DMA((4,)),
        ],
        compiler_params=params(8),
        name="pack",
    )(*held)


def stacked(refs, rows):
    return jnp.concatenate([r[rows] for r in refs], axis=0)


def pair_block(layers, tokens, left, right):
    total = None
    for l in range(layers):
        a = slice(2 * l * tokens, (2 * l + 1) * tokens)
        g = slice((2 * l + 1) * tokens, (2 * l + 2) * tokens)
        x = lax.dot_general(stacked(left, a), stacked(right, a), NT, preferred_element_type=jnp.float32)
        y = lax.dot_general(stacked(left, g), stacked(right, g), NT, preferred_element_type=jnp.float32)
        total = x * y if total is None else total + x * y
    return total.astype(jnp.bfloat16)


def lined(refs, rows):
    return jnp.concatenate([r[rows] for r in refs], axis=1)


def near_kernel(layers, tokens, count, *refs):
    own, out = refs[0], refs[count]
    k = pair_block(layers, tokens, refs[:count], [own])
    q = lined(refs[:count], slice(2 * layers * tokens, own.shape[0]))
    out[...] = lax.dot_general(q, k, NN, preferred_element_type=jnp.float32)


def near(layers, tokens, members):
    q = members[0].shape[0] - 2 * layers * tokens
    return pl.pallas_call(
        functools.partial(near_kernel, layers, tokens, len(members)),
        out_shape=jax.ShapeDtypeStruct((q, tokens), jnp.float32),
        in_specs=vmem_specs(len(members)),
        out_specs=pl.BlockSpec(memory_space=VMEM),
        compiler_params=params(8),
        cost_estimate=pair_cost(layers, tokens, members[0].shape[1], q, len(members)),
        name="near",
    )(*members)


def far_kernel(layers, tokens, count, first, *refs):
    members, visitor = refs[:count], refs[count]
    before = None if first else refs[count + 1 : 2 * count + 1]
    back, parts = refs[-count - 1], refs[-count:]
    tail = slice(2 * layers * tokens, visitor.shape[0])
    k = pair_block(layers, tokens, members, [visitor])
    back[...] = lax.dot_general(lined(members, tail), k, NN, preferred_element_type=jnp.float32)
    every = lax.dot_general(visitor[tail], k, NT, preferred_element_type=jnp.float32)
    for j in range(count):
        part = every[:, j * tokens : (j + 1) * tokens]
        parts[j][...] = part if first else before[j][...] + part


def far(layers, tokens, members, visitor, before):
    count, q = len(members), visitor.shape[0] - 2 * layers * tokens
    operands = [*members, visitor, *(before or [])]
    outs = pl.pallas_call(
        functools.partial(far_kernel, layers, tokens, count, before is None),
        out_shape=[jax.ShapeDtypeStruct((q, tokens), jnp.float32)] * (count + 1),
        in_specs=vmem_specs(len(operands)),
        out_specs=vmem_specs(count + 1),
        compiler_params=params(8),
        cost_estimate=pair_cost(layers, tokens, visitor.shape[1], 2 * q, count),
        name="far",
    )(*operands)
    return outs[0], list(outs[1:])


def split(n):
    lanes = next(j for j in (4, 2, 1) if n % j == 0)
    planes = n // lanes
    routes = []
    for shift in range(planes // 2, 0, -1):
        if 2 * shift < planes:
            routes.append([(p, (p + shift) % planes) for p in range(planes)])
        else:
            half = [(p, p + shift) for p in range(shift)]
            routes.append([(a, b) if a % 2 == 0 else (b, a) for a, b in half])
    return lanes, routes


def body(acts, grads, queries, ids):
    n = lax.axis_size("tok")
    lanes, routes = split(n)
    layers, tokens = ids.shape[0], acts.shape[1]

    def across(x, lane):
        return lax.ppermute(x, "tok", [(i, i ^ lane) for i in range(n)])

    def along(x, pairs):
        route = [(a * lanes + j, b * lanes + j) for a, b in pairs for j in range(lanes)]
        return lax.ppermute(x, "tok", route)

    mine = pack(ids, acts, grads, queries)
    visitors = [along(mine, r) for r in routes]
    members = [mine]
    if lanes > 1:
        members.append(across(mine, 1))
    if lanes > 2:
        other = across(mine, 2)
        members += [other, across(other, 1)]

    total = near(layers, tokens, members)
    parts, returned = None, []
    for visitor, route in zip(visitors, routes):
        back, parts = far(layers, tokens, members, visitor, parts)
        returned.append(along(back, [(b, a) for a, b in route]))
    if parts is None:
        return total
    if lanes == 1:
        total = total + parts[0]
    elif lanes == 2:
        total = total + parts[0]
        returned.append(across(parts[1], 1))
    else:
        total = total + parts[0]
        returned += [across(parts[j], k) for j, k in ((2, 2), (3, 3), (1, 1))]
    for r in returned:
        total = total + r
    return total


def solution(mesh):
    return jax.shard_map(
        body,
        mesh=mesh,
        in_specs=(
            P(None, ("groups", "tok"), None),
            P(None, ("groups", "tok"), None),
            P(None, ("groups", "tok")),
            P(),
        ),
        out_specs=P(None, ("groups", "tok")),
        check_vma=False,
    )
```

time: 34.5 us -> 31.2 us (0.904)
  waiting for transfers between devices: 9.08 us -> 14 us
  starting transfers between devices: 17.2 us -> 13.5 us
  local copies, waits for them, and re-layouts: 3.27 us -> 0 us
  Pallas kernels: 4.02 us -> 2.68 us
    ppermute x4, waiting for transfers between devices: 8.31 us -> 12.4 us  [along(): return lax.ppermute(x, 'tok', route)]
    ppermute x4, starting transfers between devices: 12 us -> 8.34 us  [along(): return lax.ppermute(x, 'tok', route)]
    unnamed x8 -> x0, local copies, waits for them, and re-layouts: 3.27 us -> none
    pallas_call x2, Pallas kernels: 2.47 us -> 1.1 us  [far(): pl.pallas_call(functools.partial(far_kernel, layers, tokens, count, befor...]
    ppermute x6, waiting for transfers between devices: 0.76 us -> 1.66 us  [across(): return lax.ppermute(x, 'tok', [(i, i ^ lane) for i in range(n)])]
    pallas_call x1, Pallas kernels: 0.56 us -> 1.08 us  [pack(): pl.pallas_call(pack_kernel, out_shape=jax.ShapeDtypeStruct((rows, acts.sh...]
    pallas_call x1, Pallas kernels: 1 us -> 0.5 us  [near(): pl.pallas_call(functools.partial(near_kernel, layers, tokens, len(members...]
  transfers between devices with their start and end apart: 10 -> 10, of which waited for: 4 -> 5; matrix products, arithmetic and copies ran while one was open for 0% -> 0% of each run, Pallas kernels for 6% -> 3%
where the time goes in v2:
time: 31.2 us; the launch traced here: 31 us
  waiting for transfers between devices  14 us (45%)
  starting transfers between devices  13.5 us (43%)
  Pallas kernels  2.68 us (9%)
  other arithmetic  0.63 us (2%)
    ppermute x4, waiting for transfers between devices, along(): return lax.ppermute(x, 'tok', route)  12.4 us
    ppermute x4, starting transfers between devices, along(): return lax.ppermute(x, 'tok', route)  8.34 us
    ppermute x6, starting transfers between devices, across(): return lax.ppermute(x, 'tok', [(i, i ^ lane) for i in range(n)])  5.21 us
    ppermute x6, waiting for transfers between devices, across(): return lax.ppermute(x, 'tok', [(i, i ^ lane) for i in range(n)])  1.66 us
    pallas_call x2, Pallas kernels, far(): pl.pallas_call(functools.partial(far_kernel, layers, tokens, count, befor...  1.1 us
    pallas_call x1, Pallas kernels, pack(): pl.pallas_call(pack_kernel, out_shape=jax.ShapeDtypeStruct((rows, acts.sh...  1.08 us
    add x1, other arithmetic, body(): total = total + r  0.63 us
  transfers between devices with their start and end apart: 10, of which 5 were waited for; matrix products, arithmetic and copies ran while one was open for 0% of the time, Pallas kernels for 3%

profile of v2, /device:TPU:0, one launch (start us, length us, event | category | flops | bytes accessed | tf_op | source)
XLA Modules:
  0.0 31.0 jit_solution(1272404163084941067)
XLA Ops:
  0.0 1.1 %pack.1.refs_0_ = bf16[832,128]{1,0:T(8,128)(2,1)S(1)} custom-call(s32[3]{0:T(128)} %ids_hbm.1, bf16[8,128,128]{2,1,0:T(8,128)(2,1)} %acts_hbm.1, bf16[8,128,128]{2,1,0:T(8,128)(2,1)} %grads_hbm.1, bf16[64,128]{1,0:T(8,128)(2,1)} %queries_hbm.1), custom_call_target="tpu_custom_call" | custom-call | tf_op jit(solution)/shard_map/pack/pallas_call | solution.py:50
  1.1 3.1 %collective-permute-start.1 = (bf16[832,128]{1,0:T(8,128)(2,1)S(1)}, bf16[832,128]{1,0:T(8,128)(2,1)S(1)}, u32[]{:S(2)}, u32[]{:S(2)}) collective-permute-start(bf16[832,128]{1,0:T(8,128)(2,1)S(1)} %pack.1.refs_0_), channel_id=1, source_target_pairs={{0,2},{1,3},{2,0},{3,1},{4,6},{5,7},{6,4},{7,5},{8,10},{9,11},{10,... | collective-permute-start | bytes 638984 | tf_op jit(solution)/shard_map/ppermute | solution.py:152
  4.1 0.0 collective-permute-start
  4.2 4.5 %collective-permute-start.4 = (bf16[832,128]{1,0:T(8,128)(2,1)S(1)}, bf16[832,128]{1,0:T(8,128)(2,1)S(1)}, u32[]{:S(2)}, u32[]{:S(2)}) collective-permute-start(bf16[832,128]{1,0:T(8,128)(2,1)S(1)} %pack.1.refs_0_), channel_id=1, source_target_pairs={{0,8},{1,9},{2,10},{3,11},{12,4},{13,5},{14,6},{15,7},{16,24},{17,... | collective-permute-start | bytes 638984 | tf_op jit(solution)/shard_map/ppermute | solution.py:156
  8.7 0.7 %collective-permute-done.1.refs_2_ = bf16[832,128]{1,0:T(8,128)(2,1)S(1)} collective-permute-done((bf16[832,128]{1,0:T(8,128)(2,1)S(1)}, bf16[832,128]{1,0:T(8,128)(2,1)S(1)}, u32[]{:S(2)}, u32[]{:S(2)}) %collective-permute-start.1) | collective-permute-done | bytes 213024 | tf_op jit(solution)/shard_map/ppermute | solution.py:152
  9.4 0.0 collective-permute-start.2
  9.4 1.8 %collective-permute-start.3 = (bf16[832,128]{1,0:T(8,128)(2,1)S(1)}, bf16[832,128]{1,0:T(8,128)(2,1)S(1)}, u32[]{:S(2)}, u32[]{:S(2)}) collective-permute-start(bf16[832,128]{1,0:T(8,128)(2,1)S(1)} %pack.1.refs_0_), channel_id=1, source_target_pairs={{0,4},{1,5},{2,6},{3,7},{4,8},{5,9},{6,10},{7,11},{8,12},{9,13},{1... | collective-permute-start | bytes 638984 | tf_op jit(solution)/shard_map/ppermute | solution.py:156
  11.2 0.0 collective-permute-done.refs_1_
  11.2 3.1 %collective-permute-done.4.refs_4_ = bf16[832,128]{1,0:T(8,128)(2,1)S(1)} collective-permute-done((bf16[832,128]{1,0:T(8,128)(2,1)S(1)}, bf16[832,128]{1,0:T(8,128)(2,1)S(1)}, u32[]{:S(2)}, u32[]{:S(2)}) %collective-permute-start.4) | collective-permute-done | bytes 213024 | tf_op jit(solution)/shard_map/ppermute | solution.py:156
  14.3 0.0 collective-permute-done.2.refs_3_
  14.3 0.6 %far.2 = (f32[64,128]{1,0:T(8,128)S(1)}, f32[64,128]{1,0:T(8,128)S(1)}, f32[64,128]{1,0:T(8,128)S(1)}, f32[64,128]{1,0:T(8,128)S(1)}, f32[64,128]{1,0:T(8,128)S(1)}) custom-call(bf16[832,128]{1,0:T(8,128)(2,1)S(1)} %pack.1.refs_0_, bf16[832,128]{1,0:T(8,128)(2,1)S(1)} %collective-permute-done.refs_1_, bf16[832,128]{1,0:T(8,128)(2,1)S(1)} %collective-permute-done.1.refs_2_, ...), custom_call_target="tpu_custom_call" | custom-call | flops 117440512 | bytes 917504 | tf_op jit(solution)/shard_map/far/pallas_call | solution.py:121
  14.8 5.3 %collective-permute-done.3.refs_4_ = bf16[832,128]{1,0:T(8,128)(2,1)S(1)} collective-permute-done((bf16[832,128]{1,0:T(8,128)(2,1)S(1)}, bf16[832,128]{1,0:T(8,128)(2,1)S(1)}, u32[]{:S(2)}, u32[]{:S(2)}) %collective-permute-start.3) | collective-permute-done | bytes 213024 | tf_op jit(solution)/shard_map/ppermute | solution.py:156
  20.2 0.6 %far.3 = (f32[64,128]{1,0:T(8,128)S(1)}, f32[64,128]{1,0:T(8,128)S(1)}, f32[64,128]{1,0:T(8,128)S(1)}, f32[64,128]{1,0:T(8,128)S(1)}, f32[64,128]{1,0:T(8,128)S(1)}) custom-call(bf16[832,128]{1,0:T(8,128)(2,1)S(1)} %pack.1.refs_0_, bf16[832,128]{1,0:T(8,128)(2,1)S(1)} %collective-permute-done.refs_1_, bf16[832,128]{1,0:T(8,128)(2,1)S(1)} %collective-permute-done.1.refs_2_, ...), custom_call_target="tpu_custom_call" | custom-call | flops 117440512 | bytes 917504 | tf_op jit(solution)/shard_map/far/pallas_call | solution.py:121
  20.7 0.8 %collective-permute-start.6 = (f32[64,128]{1,0:T(8,128)S(1)}, f32[64,128]{1,0:T(8,128)S(1)}, u32[]{:S(2)}, u32[]{:S(2)}) collective-permute-start(f32[64,128]{1,0:T(8,128)S(1)} %get-tuple-element.21), channel_id=1, source_target_pairs={{4,0},{5,1},{6,2},{7,3},{8,4},{9,5},{10,6},{11,7},{12,8},{13,9},{1... | collective-permute-start | bytes 98312 | tf_op jit(solution)/shard_map/ppermute | solution.py:156
  21.5 1.5 %collective-permute-start.7 = (f32[64,128]{1,0:T(8,128)S(1)}, f32[64,128]{1,0:T(8,128)S(1)}, u32[]{:S(2)}, u32[]{:S(2)}) collective-permute-start(f32[64,128]{1,0:T(8,128)S(1)} %get-tuple-element.22), channel_id=1, source_target_pairs={{0,2},{1,3},{2,0},{3,1},{4,6},{5,7},{6,4},{7,5},{8,10},{9,11},{10,... | collective-permute-start | bytes 98312 | tf_op jit(solution)/shard_map/ppermute | solution.py:152
  23.0 0.0 collective-permute-start.8
  23.0 0.6 %collective-permute-start.9 = (f32[64,128]{1,0:T(8,128)S(1)}, f32[64,128]{1,0:T(8,128)S(1)}, u32[]{:S(2)}, u32[]{:S(2)}) collective-permute-start(f32[64,128]{1,0:T(8,128)S(1)} %get-tuple-element.24), channel_id=1, source_target_pairs={{0,1},{1,0},{2,3},{3,2},{4,5},{5,4},{6,7},{7,6},{8,9},{9,8},{10,11... | collective-permute-start | bytes 98312 | tf_op jit(solution)/shard_map/ppermute | solution.py:152
  23.6 1.3 %collective-permute-start.5 = (f32[64,128]{1,0:T(8,128)S(1)}, f32[64,128]{1,0:T(8,128)S(1)}, u32[]{:S(2)}, u32[]{:S(2)}) collective-permute-start(f32[64,128]{1,0:T(8,128)S(1)} %get-tuple-element.20), channel_id=1, source_target_pairs={{8,0},{9,1},{10,2},{11,3},{4,12},{5,13},{6,14},{7,15},{24,16},{25,... | collective-permute-start | bytes 98312 | tf_op jit(solution)/shard_map/ppermute | solution.py:156
  24.9 0.5 %near.1 = f32[64,128]{1,0:T(8,128)S(1)} custom-call(bf16[832,128]{1,0:T(8,128)(2,1)S(1)} %pack.1.refs_0_, bf16[832,128]{1,0:T(8,128)(2,1)S(1)} %collective-permute-done.refs_1_, bf16[832,128]{1,0:T(8,128)(2,1)S(1)} %collective-permute-done.1.refs_2_, bf16[832,128]{1,0:T(8,128)(2,1)S(1)} %collective-permute-done.2.refs_3_), custom_call_target="tpu_custom_call" | custom-call | flops 109051904 | bytes 851968 | tf_op jit(solution)/shard_map/near/pallas_call | solution.py:94
  25.4 0.0 collective-permute-done.6
  25.5 0.9 %collective-permute-done.8 = f32[64,128]{1,0:T(8,128)S(1)} collective-permute-done((f32[64,128]{1,0:T(8,128)S(1)}, f32[64,128]{1,0:T(8,128)S(1)}, u32[]{:S(2)}, u32[]{:S(2)}) %collective-permute-start.8) | collective-permute-done | bytes 32800 | tf_op jit(solution)/shard_map/ppermute | solution.py:152
  26.4 0.0 collective-permute-done.9
  26.4 4.0 %collective-permute-done.5 = f32[64,128]{1,0:T(8,128)S(1)} collective-permute-done((f32[64,128]{1,0:T(8,128)S(1)}, f32[64,128]{1,0:T(8,128)S(1)}, u32[]{:S(2)}, u32[]{:S(2)}) %collective-permute-start.5) | collective-permute-done | bytes 32800 | tf_op jit(solution)/shard_map/ppermute | solution.py:156
  30.3 0.6 %add_add_fusion = f32[64,128]{1,0:T(8,128)} fusion(f32[64,128]{1,0:T(8,128)S(1)} %collective-permute-done.9, f32[64,128]{1,0:T(8,128)S(1)} %collective-permute-done.8, f32[64,128]{1,0:T(8,128)S(1)} %collective-permute-done.7, f32[64,128]{1,0:T(8,128)S(1)} %collective-permute-done.6, f32[64,128]{1,0:T(8,128)S(1)} %collective-permute-done.5, ...), kind=kLoop, calls=%fused_computation | loop fusion | flops 49152 | bytes 262144 | tf_op jit(solution)/shard_map/add | solution.py:183
  (1 shorter events, 0.0 us)
Async XLA Ops:
  1.1 8.3 %collective-permute-start.1 = (bf16[832,128]{1,0:T(8,128)(2,1)S(1)}, bf16[832,128]{1,0:T(8,128)(2,1)S(1)}, u32[]{:S(2)}, u32[]{:S(2)}) collective-permute-start(bf16[832,128]{1,0:T(8,128)(2,1)S(1)} %pack.1.refs_0_), channel_id=1, source_target_pairs={{0,2},{1,3},{2,0},{3,1},{4,6},{5,7},{6,4},{7,5},{8,10},{9,11},{10,... | collective-permute-start | bytes 638984 | tf_op jit(solution)/shard_map/ppermute | solution.py:152
  4.1 7.1 %collective-permute-start = (bf16[832,128]{1,0:T(8,128)(2,1)S(1)}, bf16[832,128]{1,0:T(8,128)(2,1)S(1)}, u32[]{:S(2)}, u32[]{:S(2)}) collective-permute-start(bf16[832,128]{1,0:T(8,128)(2,1)S(1)} %pack.1.refs_0_), channel_id=1, source_target_pairs={{0,1},{1,0},{2,3},{3,2},{4,5},{5,4},{6,7},{7,6},{8,9},{9,8},{10,11... | collective-permute-start | bytes 638984 | tf_op jit(solution)/shard_map/ppermute | solution.py:152
  4.2 10.1 %collective-permute-start.4 = (bf16[832,128]{1,0:T(8,128)(2,1)S(1)}, bf16[832,128]{1,0:T(8,128)(2,1)S(1)}, u32[]{:S(2)}, u32[]{:S(2)}) collective-permute-start(bf16[832,128]{1,0:T(8,128)(2,1)S(1)} %pack.1.refs_0_), channel_id=1, source_target_pairs={{0,8},{1,9},{2,10},{3,11},{12,4},{13,5},{14,6},{15,7},{16,24},{17,... | collective-permute-start | bytes 638984 | tf_op jit(solution)/shard_map/ppermute | solution.py:156
  9.4 4.9 %collective-permute-start.2 = (bf16[832,128]{1,0:T(8,128)(2,1)S(1)}, bf16[832,128]{1,0:T(8,128)(2,1)S(1)}, u32[]{:S(2)}, u32[]{:S(2)}) collective-permute-start(bf16[832,128]{1,0:T(8,128)(2,1)S(1)} %collective-permute-done.1.refs_2_), channel_id=1, source_target_pairs={{0,1},{1,0},{2,3},{3,2},{4,5},{5,4},{6,7},{7,6},{8,9},{9,8},{10,11... | collective-permute-start | bytes 638984 | tf_op jit(solution)/shard_map/ppermute | solution.py:152
  9.4 10.8 %collective-permute-start.3 = (bf16[832,128]{1,0:T(8,128)(2,1)S(1)}, bf16[832,128]{1,0:T(8,128)(2,1)S(1)}, u32[]{:S(2)}, u32[]{:S(2)}) collective-permute-start(bf16[832,128]{1,0:T(8,128)(2,1)S(1)} %pack.1.refs_0_), channel_id=1, source_target_pairs={{0,4},{1,5},{2,6},{3,7},{4,8},{5,9},{6,10},{7,11},{8,12},{9,13},{1... | collective-permute-start | bytes 638984 | tf_op jit(solution)/shard_map/ppermute | solution.py:156
  20.7 4.7 %collective-permute-start.6 = (f32[64,128]{1,0:T(8,128)S(1)}, f32[64,128]{1,0:T(8,128)S(1)}, u32[]{:S(2)}, u32[]{:S(2)}) collective-permute-start(f32[64,128]{1,0:T(8,128)S(1)} %get-tuple-element.21), channel_id=1, source_target_pairs={{4,0},{5,1},{6,2},{7,3},{8,4},{9,5},{10,6},{11,7},{12,8},{13,9},{1... | collective-permute-start | bytes 98312 | tf_op jit(solution)/shard_map/ppermute | solution.py:156
  21.5 4.0 %collective-permute-start.7 = (f32[64,128]{1,0:T(8,128)S(1)}, f32[64,128]{1,0:T(8,128)S(1)}, u32[]{:S(2)}, u32[]{:S(2)}) collective-permute-start(f32[64,128]{1,0:T(8,128)S(1)} %get-tuple-element.22), channel_id=1, source_target_pairs={{0,2},{1,3},{2,0},{3,1},{4,6},{5,7},{6,4},{7,5},{8,10},{9,11},{10,... | collective-permute-start | bytes 98312 | tf_op jit(solution)/shard_map/ppermute | solution.py:152
  23.0 3.3 %collective-permute-start.8 = (f32[64,128]{1,0:T(8,128)S(1)}, f32[64,128]{1,0:T(8,128)S(1)}, u32[]{:S(2)}, u32[]{:S(2)}) collective-permute-start(f32[64,128]{1,0:T(8,128)S(1)} %get-tuple-element.23), channel_id=1, source_target_pairs={{0,3},{1,2},{2,1},{3,0},{4,7},{5,6},{6,5},{7,4},{8,11},{9,10},{10,... | collective-permute-start | bytes 98312 | tf_op jit(solution)/shard_map/ppermute | solution.py:152
  23.0 3.3 %collective-permute-start.9 = (f32[64,128]{1,0:T(8,128)S(1)}, f32[64,128]{1,0:T(8,128)S(1)}, u32[]{:S(2)}, u32[]{:S(2)}) collective-permute-start(f32[64,128]{1,0:T(8,128)S(1)} %get-tuple-element.24), channel_id=1, source_target_pairs={{0,1},{1,0},{2,3},{3,2},{4,5},{5,4},{6,7},{7,6},{8,9},{9,8},{10,11... | collective-permute-start | bytes 98312 | tf_op jit(solution)/shard_map/ppermute | solution.py:152
  23.6 6.7 %collective-permute-start.5 = (f32[64,128]{1,0:T(8,128)S(1)}, f32[64,128]{1,0:T(8,128)S(1)}, u32[]{:S(2)}, u32[]{:S(2)}) collective-permute-start(f32[64,128]{1,0:T(8,128)S(1)} %get-tuple-element.20), channel_id=1, source_target_pairs={{8,0},{9,1},{10,2},{11,3},{4,12},{5,13},{6,14},{7,15},{24,16},{25,... | collective-permute-start | bytes 98312 | tf_op jit(solution)/shard_map/ppermute | solution.py:156

commit v3 on v2

--- a/solution.py
+++ b/solution.py
@@ -134,7 +134,7 @@
     lanes = next(j for j in (4, 2, 1) if n % j == 0)
     planes = n // lanes
     routes = []
-    for shift in range(planes // 2, 0, -1):
+    for shift in range(1, planes // 2 + 1):
         if 2 * shift < planes:
             routes.append([(p, (p + shift) % planes) for p in range(planes)])
         else:
@@ -177,8 +177,9 @@
         total = total + parts[0]
         returned.append(across(parts[1], 1))
     else:
-        total = total + parts[0]
-        returned += [across(parts[j], k) for j, k in ((2, 2), (3, 3), (1, 1))]
+        met = across(jnp.stack([parts[1], parts[3]]), 1)
+        total = total + parts[0] + met[0]
+        returned.append(across(parts[2] + met[1], 2))
     for r in returned:
         total = total + r
     return total

time: 31.2 us -> 27.8 us (0.89)
  waiting for transfers between devices: 14 us -> 10.5 us
    ppermute x4, waiting for transfers between devices: 12.4 us -> 6.82 us  [along(): return lax.ppermute(x, 'tok', route)]
    ppermute x6 -> x5, waiting for transfers between devices: 1.66 us -> 3.68 us  [across(): return lax.ppermute(x, 'tok', [(i, i ^ lane) for i in range(n)])]
    ppermute x4, starting transfers between devices: 8.34 us -> 8.98 us  [along(): return lax.ppermute(x, 'tok', route)]
    ppermute x6 -> x5, starting transfers between devices: 5.21 us -> 4.72 us  [across(): return lax.ppermute(x, 'tok', [(i, i ^ lane) for i in range(n)])]
  transfers between devices with their start and end apart: 10 -> 9, of which waited for: 5 -> 3; matrix products, arithmetic and copies ran while one was open for 0% -> 0% of each run, Pallas kernels for 3% -> 4%
where the time goes in v3:
time: 27.8 us; the launch traced here: 27.6 us
  starting transfers between devices  13.7 us (49%)
  waiting for transfers between devices  10.5 us (38%)
  Pallas kernels  2.68 us (10%)
  other arithmetic  0.64 us (2%)
    ppermute x4, starting transfers between devices, along(): return lax.ppermute(x, 'tok', route)  8.98 us
    ppermute x4, waiting for transfers between devices, along(): return lax.ppermute(x, 'tok', route)  6.82 us
    ppermute x5, starting transfers between devices, across(): return lax.ppermute(x, 'tok', [(i, i ^ lane) for i in range(n)])  4.72 us
    ppermute x5, waiting for transfers between devices, across(): return lax.ppermute(x, 'tok', [(i, i ^ lane) for i in range(n)])  3.68 us
    pallas_call x2, Pallas kernels, far(): pl.pallas_call(functools.partial(far_kernel, layers, tokens, count, befor...  1.11 us
    pallas_call x1, Pallas kernels, pack(): pl.pallas_call(pack_kernel, out_shape=jax.ShapeDtypeStruct((rows, acts.sh...  1.08 us
    add x1, other arithmetic, body(): total = total + r  0.63 us
  transfers between devices with their start and end apart: 9, of which 3 were waited for; matrix products, arithmetic and copies ran while one was open for 0% of the time, Pallas kernels for 4%

profile of v3, /device:TPU:0, one launch (start us, length us, event | category | flops | bytes accessed | tf_op | source)
XLA Modules:
  0.0 27.6 jit_solution(8231121771314212369)
XLA Ops:
  0.0 1.1 %pack.1.refs_0_ = bf16[832,128]{1,0:T(8,128)(2,1)S(1)} custom-call(s32[3]{0:T(128)} %ids_hbm.1, bf16[8,128,128]{2,1,0:T(8,128)(2,1)} %acts_hbm.1, bf16[8,128,128]{2,1,0:T(8,128)(2,1)} %grads_hbm.1, bf16[64,128]{1,0:T(8,128)(2,1)} %queries_hbm.1), custom_call_target="tpu_custom_call" | custom-call | tf_op jit(solution)/shard_map/pack/pallas_call | solution.py:50
  1.1 3.1 %collective-permute-start.1 = (bf16[832,128]{1,0:T(8,128)(2,1)S(1)}, bf16[832,128]{1,0:T(8,128)(2,1)S(1)}, u32[]{:S(2)}, u32[]{:S(2)}) collective-permute-start(bf16[832,128]{1,0:T(8,128)(2,1)S(1)} %pack.1.refs_0_), channel_id=1, source_target_pairs={{0,2},{1,3},{2,0},{3,1},{4,6},{5,7},{6,4},{7,5},{8,10},{9,11},{10,... | collective-permute-start | bytes 638984 | tf_op jit(solution)/shard_map/ppermute | solution.py:152
  4.1 0.0 collective-permute-start
  4.2 1.6 %collective-permute-start.4 = (bf16[832,128]{1,0:T(8,128)(2,1)S(1)}, bf16[832,128]{1,0:T(8,128)(2,1)S(1)}, u32[]{:S(2)}, u32[]{:S(2)}) collective-permute-start(bf16[832,128]{1,0:T(8,128)(2,1)S(1)} %pack.1.refs_0_), channel_id=1, source_target_pairs={{0,4},{1,5},{2,6},{3,7},{4,8},{5,9},{6,10},{7,11},{8,12},{9,13},{1... | collective-permute-start | bytes 638984 | tf_op jit(solution)/shard_map/ppermute | solution.py:156
  5.7 3.7 %collective-permute-done.1.refs_2_ = bf16[832,128]{1,0:T(8,128)(2,1)S(1)} collective-permute-done((bf16[832,128]{1,0:T(8,128)(2,1)S(1)}, bf16[832,128]{1,0:T(8,128)(2,1)S(1)}, u32[]{:S(2)}, u32[]{:S(2)}) %collective-permute-start.1) | collective-permute-done | bytes 213024 | tf_op jit(solution)/shard_map/ppermute | solution.py:152
  9.4 0.0 collective-permute-start.2
  9.4 4.7 %collective-permute-start.3 = (bf16[832,128]{1,0:T(8,128)(2,1)S(1)}, bf16[832,128]{1,0:T(8,128)(2,1)S(1)}, u32[]{:S(2)}, u32[]{:S(2)}) collective-permute-start(bf16[832,128]{1,0:T(8,128)(2,1)S(1)} %pack.1.refs_0_), channel_id=1, source_target_pairs={{0,8},{1,9},{2,10},{3,11},{12,4},{13,5},{14,6},{15,7},{16,24},{17,... | collective-permute-start | bytes 638984 | tf_op jit(solution)/shard_map/ppermute | solution.py:156
  14.1 0.0 collective-permute-done.refs_1_
  14.1 0.0 collective-permute-done.4.refs_4_
  14.1 0.0 collective-permute-done.2.refs_3_
  14.2 0.6 %far.2 = (f32[64,128]{1,0:T(8,128)S(1)}, f32[64,128]{1,0:T(8,128)S(1)}, f32[64,128]{1,0:T(8,128)S(1)}, f32[64,128]{1,0:T(8,128)S(1)}, f32[64,128]{1,0:T(8,128)S(1)}) custom-call(bf16[832,128]{1,0:T(8,128)(2,1)S(1)} %pack.1.refs_0_, bf16[832,128]{1,0:T(8,128)(2,1)S(1)} %collective-permute-done.refs_1_, bf16[832,128]{1,0:T(8,128)(2,1)S(1)} %collective-permute-done.1.refs_2_, ...), custom_call_target="tpu_custom_call" | custom-call | flops 117440512 | bytes 917504 | tf_op jit(solution)/shard_map/far/pallas_call | solution.py:121
  14.7 4.6 %collective-permute-done.3.refs_4_ = bf16[832,128]{1,0:T(8,128)(2,1)S(1)} collective-permute-done((bf16[832,128]{1,0:T(8,128)(2,1)S(1)}, bf16[832,128]{1,0:T(8,128)(2,1)S(1)}, u32[]{:S(2)}, u32[]{:S(2)}) %collective-permute-start.3) | collective-permute-done | bytes 213024 | tf_op jit(solution)/shard_map/ppermute | solution.py:156
  19.3 0.6 %far.3 = (f32[64,128]{1,0:T(8,128)S(1)}, f32[64,128]{1,0:T(8,128)S(1)}, f32[64,128]{1,0:T(8,128)S(1)}, f32[64,128]{1,0:T(8,128)S(1)}, f32[64,128]{1,0:T(8,128)S(1)}) custom-call(bf16[832,128]{1,0:T(8,128)(2,1)S(1)} %pack.1.refs_0_, bf16[832,128]{1,0:T(8,128)(2,1)S(1)} %collective-permute-done.refs_1_, bf16[832,128]{1,0:T(8,128)(2,1)S(1)} %collective-permute-done.1.refs_2_, ...), custom_call_target="tpu_custom_call" | custom-call | flops 117440512 | bytes 917504 | tf_op jit(solution)/shard_map/far/pallas_call | solution.py:121
  19.9 0.1 collective-permute-start.5
  19.9 1.3 %collective-permute-start.7 = (f32[64,128]{1,0:T(8,128)S(1)}, f32[64,128]{1,0:T(8,128)S(1)}, u32[]{:S(2)}, u32[]{:S(2)}) collective-permute-start(f32[64,128]{1,0:T(8,128)S(1)} %get-tuple-element.23), channel_id=1, source_target_pairs={{8,0},{9,1},{10,2},{11,3},{4,12},{5,13},{6,14},{7,15},{24,16},{25,... | collective-permute-start | bytes 98312 | tf_op jit(solution)/shard_map/ppermute | solution.py:156
  21.2 1.4 %collective-permute-start.6 = (f32[64,128]{1,0:T(8,128)S(1)}, f32[64,128]{1,0:T(8,128)S(1)}, u32[]{:S(2)}, u32[]{:S(2)}) collective-permute-start(f32[64,128]{1,0:T(8,128)S(1)} %get-tuple-element.22), channel_id=1, source_target_pairs={{4,0},{5,1},{6,2},{7,3},{8,4},{9,5},{10,6},{11,7},{12,8},{13,9},{1... | collective-permute-start | bytes 98312 | tf_op jit(solution)/shard_map/ppermute | solution.py:156
  22.6 0.0 collective-permute-done.5
  22.6 1.6 %collective-permute-start.8 = (f32[64,128]{1,0:T(8,128)S(1)}, f32[64,128]{1,0:T(8,128)S(1)}, u32[]{:S(2)}, u32[]{:S(2)}) collective-permute-start(f32[64,128]{1,0:T(8,128)S(1)} %fusion), channel_id=1, source_target_pairs={{0,2},{1,3},{2,0},{3,1},{4,6},{5,7},{6,4},{7,5},{8,10},{9,11},{10,... | collective-permute-start | bytes 98312 | tf_op jit(solution)/shard_map/ppermute | solution.py:152
  24.2 0.5 %near.1 = f32[64,128]{1,0:T(8,128)S(1)} custom-call(bf16[832,128]{1,0:T(8,128)(2,1)S(1)} %pack.1.refs_0_, bf16[832,128]{1,0:T(8,128)(2,1)S(1)} %collective-permute-done.refs_1_, bf16[832,128]{1,0:T(8,128)(2,1)S(1)} %collective-permute-done.1.refs_2_, bf16[832,128]{1,0:T(8,128)(2,1)S(1)} %collective-permute-done.2.refs_3_), custom_call_target="tpu_custom_call" | custom-call | flops 109051904 | bytes 851968 | tf_op jit(solution)/shard_map/near/pallas_call | solution.py:94
  24.7 2.2 %collective-permute-done.7 = f32[64,128]{1,0:T(8,128)S(1)} collective-permute-done((f32[64,128]{1,0:T(8,128)S(1)}, f32[64,128]{1,0:T(8,128)S(1)}, u32[]{:S(2)}, u32[]{:S(2)}) %collective-permute-start.7) | collective-permute-done | bytes 32800 | tf_op jit(solution)/shard_map/ppermute | solution.py:156
  27.0 0.0 collective-permute-done.6
  27.0 0.0 collective-permute-done.8
  27.0 0.6 %fusion.4 = f32[64,128]{1,0:T(8,128)} fusion(f32[64,128]{1,0:T(8,128)S(1)} %collective-permute-done.8, f32[64,128]{1,0:T(8,128)S(1)} %collective-permute-done.7, f32[64,128]{1,0:T(8,128)S(1)} %collective-permute-done.6, f32[2,64,128]{2,1,0:T(8,128)S(1)} %collective-permute-done.5, f32[64,128]{1,0:T(8,128)S(1)} %near.1, f32[64,128]{1,0:T(8,128)S(1)} %get-tuple-element.19), kind=kLoop, calls=%fused_computation.7 | loop fusion | flops 40960 | bytes 229376 | tf_op jit(solution)/shard_map/add | solution.py:184
  (2 shorter events, 0.0 us)
Async XLA Ops:
  1.1 8.3 %collective-permute-start.1 = (bf16[832,128]{1,0:T(8,128)(2,1)S(1)}, bf16[832,128]{1,0:T(8,128)(2,1)S(1)}, u32[]{:S(2)}, u32[]{:S(2)}) collective-permute-start(bf16[832,128]{1,0:T(8,128)(2,1)S(1)} %pack.1.refs_0_), channel_id=1, source_target_pairs={{0,2},{1,3},{2,0},{3,1},{4,6},{5,7},{6,4},{7,5},{8,10},{9,11},{10,... | collective-permute-start | bytes 638984 | tf_op jit(solution)/shard_map/ppermute | solution.py:152
  4.1 10.0 %collective-permute-start = (bf16[832,128]{1,0:T(8,128)(2,1)S(1)}, bf16[832,128]{1,0:T(8,128)(2,1)S(1)}, u32[]{:S(2)}, u32[]{:S(2)}) collective-permute-start(bf16[832,128]{1,0:T(8,128)(2,1)S(1)} %pack.1.refs_0_), channel_id=1, source_target_pairs={{0,1},{1,0},{2,3},{3,2},{4,5},{5,4},{6,7},{7,6},{8,9},{9,8},{10,11... | collective-permute-start | bytes 638984 | tf_op jit(solution)/shard_map/ppermute | solution.py:152
  4.2 10.0 %collective-permute-start.4 = (bf16[832,128]{1,0:T(8,128)(2,1)S(1)}, bf16[832,128]{1,0:T(8,128)(2,1)S(1)}, u32[]{:S(2)}, u32[]{:S(2)}) collective-permute-start(bf16[832,128]{1,0:T(8,128)(2,1)S(1)} %pack.1.refs_0_), channel_id=1, source_target_pairs={{0,4},{1,5},{2,6},{3,7},{4,8},{5,9},{6,10},{7,11},{8,12},{9,13},{1... | collective-permute-start | bytes 638984 | tf_op jit(solution)/shard_map/ppermute | solution.py:156
  9.4 4.8 %collective-permute-start.2 = (bf16[832,128]{1,0:T(8,128)(2,1)S(1)}, bf16[832,128]{1,0:T(8,128)(2,1)S(1)}, u32[]{:S(2)}, u32[]{:S(2)}) collective-permute-start(bf16[832,128]{1,0:T(8,128)(2,1)S(1)} %collective-permute-done.1.refs_2_), channel_id=1, source_target_pairs={{0,1},{1,0},{2,3},{3,2},{4,5},{5,4},{6,7},{7,6},{8,9},{9,8},{10,11... | collective-permute-start | bytes 638984 | tf_op jit(solution)/shard_map/ppermute | solution.py:152
  9.4 9.9 %collective-permute-start.3 = (bf16[832,128]{1,0:T(8,128)(2,1)S(1)}, bf16[832,128]{1,0:T(8,128)(2,1)S(1)}, u32[]{:S(2)}, u32[]{:S(2)}) collective-permute-start(bf16[832,128]{1,0:T(8,128)(2,1)S(1)} %pack.1.refs_0_), channel_id=1, source_target_pairs={{0,8},{1,9},{2,10},{3,11},{12,4},{13,5},{14,6},{15,7},{16,24},{17,... | collective-permute-start | bytes 638984 | tf_op jit(solution)/shard_map/ppermute | solution.py:156
  19.9 2.8 %collective-permute-start.5 = (f32[2,64,128]{2,1,0:T(8,128)S(1)}, f32[2,64,128]{2,1,0:T(8,128)S(1)}, u32[]{:S(2)}, u32[]{:S(2)}) collective-permute-start(f32[2,64,128]{2,1,0:T(8,128)S(1)} %pad_maximum_fusion), channel_id=1, source_target_pairs={{0,1},{1,0},{2,3},{3,2},{4,5},{5,4},{6,7},{7,6},{8,9},{9,8},{10,11... | collective-permute-start | bytes 196616 | tf_op jit(solution)/shard_map/ppermute | solution.py:152
  19.9 7.0 %collective-permute-start.7 = (f32[64,128]{1,0:T(8,128)S(1)}, f32[64,128]{1,0:T(8,128)S(1)}, u32[]{:S(2)}, u32[]{:S(2)}) collective-permute-start(f32[64,128]{1,0:T(8,128)S(1)} %get-tuple-element.23), channel_id=1, source_target_pairs={{8,0},{9,1},{10,2},{11,3},{4,12},{5,13},{6,14},{7,15},{24,16},{25,... | collective-permute-start | bytes 98312 | tf_op jit(solution)/shard_map/ppermute | solution.py:156
  21.2 5.8 %collective-permute-start.6 = (f32[64,128]{1,0:T(8,128)S(1)}, f32[64,128]{1,0:T(8,128)S(1)}, u32[]{:S(2)}, u32[]{:S(2)}) collective-permute-start(f32[64,128]{1,0:T(8,128)S(1)} %get-tuple-element.22), channel_id=1, source_target_pairs={{4,0},{5,1},{6,2},{7,3},{8,4},{9,5},{10,6},{11,7},{12,8},{13,9},{1... | collective-permute-start | bytes 98312 | tf_op jit(solution)/shard_map/ppermute | solution.py:156
  22.6 4.3 %collective-permute-start.8 = (f32[64,128]{1,0:T(8,128)S(1)}, f32[64,128]{1,0:T(8,128)S(1)}, u32[]{:S(2)}, u32[]{:S(2)}) collective-permute-start(f32[64,128]{1,0:T(8,128)S(1)} %fusion), channel_id=1, source_target_pairs={{0,2},{1,3},{2,0},{3,1},{4,6},{5,7},{6,4},{7,5},{8,10},{9,11},{10,... | collective-permute-start | bytes 98312 | tf_op jit(solution)/shard_map/ppermute | solution.py:152

commit v4 on v3

--- a/solution.py
+++ b/solution.py
@@ -143,16 +143,24 @@
     return lanes, routes
 
 
+def filled(pairs, planes):
+    idle = [p for p in range(planes) if p not in [a for a, _ in pairs]]
+    bare = [p for p in range(planes) if p not in [b for _, b in pairs]]
+    return pairs + list(zip(idle, bare))
+
+
 def body(acts, grads, queries, ids):
     n = lax.axis_size("tok")
     lanes, routes = split(n)
+    planes = n // lanes
     layers, tokens = ids.shape[0], acts.shape[1]
 
     def across(x, lane):
         return lax.ppermute(x, "tok", [(i, i ^ lane) for i in range(n)])
 
     def along(x, pairs):
-        route = [(a * lanes + j, b * lanes + j) for a, b in pairs for j in range(lanes)]
+        flip = min(1, lanes - 1)
+        route = [(a * lanes + j, b * lanes + (j ^ flip)) for a, b in pairs for j in range(lanes)]
         return lax.ppermute(x, "tok", route)
 
     mine = pack(ids, acts, grads, queries)
@@ -168,7 +176,7 @@
     parts, returned = None, []
     for visitor, route in zip(visitors, routes):
         back, parts = far(layers, tokens, members, visitor, parts)
-        returned.append(along(back, [(b, a) for a, b in route]))
+        returned.append(along(back, filled([(b, a) for a, b in route], planes)))
     if parts is None:
         return total
     if lanes == 1:

time: 27.8 us -> 29 us (1.043)
  starting transfers between devices: 13.7 us -> 15.6 us
  waiting for transfers between devices: 10.5 us -> 9.78 us
    ppermute x4, waiting for transfers between devices: 6.82 us -> 4.35 us  [along(): return lax.ppermute(x, 'tok', route)]
    ppermute x4, starting transfers between devices: 8.98 us -> 10.9 us  [along(): return lax.ppermute(x, 'tok', route)]
    ppermute x5, waiting for transfers between devices: 3.68 us -> 5.43 us  [across(): return lax.ppermute(x, 'tok', [(i, i ^ lane) for i in range(n)])]
where the time goes in v4:
time: 29 us; the launch traced here: 28.8 us
  starting transfers between devices  15.6 us (54%)
  waiting for transfers between devices  9.78 us (34%)
  Pallas kernels  2.69 us (9%)
  other arithmetic  0.64 us (2%)
    ppermute x4, starting transfers between devices, along(): return lax.ppermute(x, 'tok', route)  10.9 us
    ppermute x5, waiting for transfers between devices, across(): return lax.ppermute(x, 'tok', [(i, i ^ lane) for i in range(n)])  5.43 us
    ppermute x5, starting transfers between devices, across(): return lax.ppermute(x, 'tok', [(i, i ^ lane) for i in range(n)])  4.72 us
    ppermute x4, waiting for transfers between devices, along(): return lax.ppermute(x, 'tok', route)  4.35 us
    pallas_call x2, Pallas kernels, far(): pl.pallas_call(functools.partial(far_kernel, layers, tokens, count, befor...  1.11 us
    pallas_call x1, Pallas kernels, pack(): pl.pallas_call(pack_kernel, out_shape=jax.ShapeDtypeStruct((rows, acts.sh...  1.08 us
    add x1, other arithmetic, body(): total = total + r  0.63 us
  transfers between devices with their start and end apart: 9, of which 3 were waited for; matrix products, arithmetic and copies ran while one was open for 0% of the time, Pallas kernels for 4%

profile of v4, /device:TPU:0, one launch (start us, length us, event | category | flops | bytes accessed | tf_op | source)
XLA Modules:
  0.0 28.8 jit_solution(6463692946550049091)
XLA Ops:
  0.0 1.1 %pack.1.refs_0_ = bf16[832,128]{1,0:T(8,128)(2,1)S(1)} custom-call(s32[3]{0:T(128)} %ids_hbm.1, bf16[8,128,128]{2,1,0:T(8,128)(2,1)} %acts_hbm.1, bf16[8,128,128]{2,1,0:T(8,128)(2,1)} %grads_hbm.1, bf16[64,128]{1,0:T(8,128)(2,1)} %queries_hbm.1), custom_call_target="tpu_custom_call" | custom-call | tf_op jit(solution)/shard_map/pack/pallas_call | solution.py:50
  1.1 3.1 %collective-permute-start.1 = (bf16[832,128]{1,0:T(8,128)(2,1)S(1)}, bf16[832,128]{1,0:T(8,128)(2,1)S(1)}, u32[]{:S(2)}, u32[]{:S(2)}) collective-permute-start(bf16[832,128]{1,0:T(8,128)(2,1)S(1)} %pack.1.refs_0_), channel_id=1, source_target_pairs={{0,2},{1,3},{2,0},{3,1},{4,6},{5,7},{6,4},{7,5},{8,10},{9,11},{10,... | collective-permute-start | bytes 638984 | tf_op jit(solution)/shard_map/ppermute | solution.py:159
  4.1 0.0 collective-permute-start
  4.2 1.7 %collective-permute-start.4 = (bf16[832,128]{1,0:T(8,128)(2,1)S(1)}, bf16[832,128]{1,0:T(8,128)(2,1)S(1)}, u32[]{:S(2)}, u32[]{:S(2)}) collective-permute-start(bf16[832,128]{1,0:T(8,128)(2,1)S(1)} %pack.1.refs_0_), channel_id=1, source_target_pairs={{0,5},{1,4},{2,7},{3,6},{4,9},{5,8},{6,11},{7,10},{8,13},{9,12},{1... | collective-permute-start | bytes 638984 | tf_op jit(solution)/shard_map/ppermute | solution.py:164
  5.8 3.6 %collective-permute-done.1.refs_2_ = bf16[832,128]{1,0:T(8,128)(2,1)S(1)} collective-permute-done((bf16[832,128]{1,0:T(8,128)(2,1)S(1)}, bf16[832,128]{1,0:T(8,128)(2,1)S(1)}, u32[]{:S(2)}, u32[]{:S(2)}) %collective-permute-start.1) | collective-permute-done | bytes 213024 | tf_op jit(solution)/shard_map/ppermute | solution.py:159
  9.4 0.0 collective-permute-start.2
  9.4 4.8 %collective-permute-start.3 = (bf16[832,128]{1,0:T(8,128)(2,1)S(1)}, bf16[832,128]{1,0:T(8,128)(2,1)S(1)}, u32[]{:S(2)}, u32[]{:S(2)}) collective-permute-start(bf16[832,128]{1,0:T(8,128)(2,1)S(1)} %pack.1.refs_0_), channel_id=1, source_target_pairs={{0,9},{1,8},{2,11},{3,10},{12,5},{13,4},{14,7},{15,6},{16,25},{17,... | collective-permute-start | bytes 638984 | tf_op jit(solution)/shard_map/ppermute | solution.py:164
  14.2 0.0 collective-permute-done.refs_1_
  14.2 0.0 collective-permute-done.4.refs_4_
  14.3 0.0 collective-permute-done.2.refs_3_
  14.3 0.6 %far.2 = (f32[64,128]{1,0:T(8,128)S(1)}, f32[64,128]{1,0:T(8,128)S(1)}, f32[64,128]{1,0:T(8,128)S(1)}, f32[64,128]{1,0:T(8,128)S(1)}, f32[64,128]{1,0:T(8,128)S(1)}) custom-call(bf16[832,128]{1,0:T(8,128)(2,1)S(1)} %pack.1.refs_0_, bf16[832,128]{1,0:T(8,128)(2,1)S(1)} %collective-permute-done.refs_1_, bf16[832,128]{1,0:T(8,128)(2,1)S(1)} %collective-permute-done.1.refs_2_, ...), custom_call_target="tpu_custom_call" | custom-call | flops 117440512 | bytes 917504 | tf_op jit(solution)/shard_map/far/pallas_call | solution.py:121
  14.8 4.3 %collective-permute-done.3.refs_4_ = bf16[832,128]{1,0:T(8,128)(2,1)S(1)} collective-permute-done((bf16[832,128]{1,0:T(8,128)(2,1)S(1)}, bf16[832,128]{1,0:T(8,128)(2,1)S(1)}, u32[]{:S(2)}, u32[]{:S(2)}) %collective-permute-start.3) | collective-permute-done | bytes 213024 | tf_op jit(solution)/shard_map/ppermute | solution.py:164
  19.2 0.6 %far.3 = (f32[64,128]{1,0:T(8,128)S(1)}, f32[64,128]{1,0:T(8,128)S(1)}, f32[64,128]{1,0:T(8,128)S(1)}, f32[64,128]{1,0:T(8,128)S(1)}, f32[64,128]{1,0:T(8,128)S(1)}) custom-call(bf16[832,128]{1,0:T(8,128)(2,1)S(1)} %pack.1.refs_0_, bf16[832,128]{1,0:T(8,128)(2,1)S(1)} %collective-permute-done.refs_1_, bf16[832,128]{1,0:T(8,128)(2,1)S(1)} %collective-permute-done.1.refs_2_, ...), custom_call_target="tpu_custom_call" | custom-call | flops 117440512 | bytes 917504 | tf_op jit(solution)/shard_map/far/pallas_call | solution.py:121
  19.7 0.1 collective-permute-start.5
  19.8 1.8 %collective-permute-start.7 = (f32[64,128]{1,0:T(8,128)S(1)}, f32[64,128]{1,0:T(8,128)S(1)}, u32[]{:S(2)}, u32[]{:S(2)}) collective-permute-start(f32[64,128]{1,0:T(8,128)S(1)} %get-tuple-element.23), channel_id=1, source_target_pairs={{8,1},{9,0},{10,3},{11,2},{4,13},{5,12},{6,15},{7,14},{0,5},{1,4},... | collective-permute-start | bytes 98312 | tf_op jit(solution)/shard_map/ppermute | solution.py:164
  21.7 2.5 %collective-permute-start.6 = (f32[64,128]{1,0:T(8,128)S(1)}, f32[64,128]{1,0:T(8,128)S(1)}, u32[]{:S(2)}, u32[]{:S(2)}) collective-permute-start(f32[64,128]{1,0:T(8,128)S(1)} %get-tuple-element.22), channel_id=1, source_target_pairs={{4,1},{5,0},{6,3},{7,2},{8,5},{9,4},{10,7},{11,6},{12,9},{13,8},{1... | collective-permute-start | bytes 98312 | tf_op jit(solution)/shard_map/ppermute | solution.py:164
  24.2 0.0 collective-permute-done.5
  24.2 1.6 %collective-permute-start.8 = (f32[64,128]{1,0:T(8,128)S(1)}, f32[64,128]{1,0:T(8,128)S(1)}, u32[]{:S(2)}, u32[]{:S(2)}) collective-permute-start(f32[64,128]{1,0:T(8,128)S(1)} %fusion), channel_id=1, source_target_pairs={{0,2},{1,3},{2,0},{3,1},{4,6},{5,7},{6,4},{7,5},{8,10},{9,11},{10,... | collective-permute-start | bytes 98312 | tf_op jit(solution)/shard_map/ppermute | solution.py:159
  25.8 0.5 %near.1 = f32[64,128]{1,0:T(8,128)S(1)} custom-call(bf16[832,128]{1,0:T(8,128)(2,1)S(1)} %pack.1.refs_0_, bf16[832,128]{1,0:T(8,128)(2,1)S(1)} %collective-permute-done.refs_1_, bf16[832,128]{1,0:T(8,128)(2,1)S(1)} %collective-permute-done.1.refs_2_, bf16[832,128]{1,0:T(8,128)(2,1)S(1)} %collective-permute-done.2.refs_3_), custom_call_target="tpu_custom_call" | custom-call | flops 109051904 | bytes 851968 | tf_op jit(solution)/shard_map/near/pallas_call | solution.py:94
  26.3 0.0 collective-permute-done.7
  26.3 0.0 collective-permute-done.6
  26.3 1.9 %collective-permute-done.8 = f32[64,128]{1,0:T(8,128)S(1)} collective-permute-done((f32[64,128]{1,0:T(8,128)S(1)}, f32[64,128]{1,0:T(8,128)S(1)}, u32[]{:S(2)}, u32[]{:S(2)}) %collective-permute-start.8) | collective-permute-done | bytes 32800 | tf_op jit(solution)/shard_map/ppermute | solution.py:159
  28.2 0.6 %fusion.4 = f32[64,128]{1,0:T(8,128)} fusion(f32[64,128]{1,0:T(8,128)S(1)} %collective-permute-done.8, f32[64,128]{1,0:T(8,128)S(1)} %collective-permute-done.7, f32[64,128]{1,0:T(8,128)S(1)} %collective-permute-done.6, f32[2,64,128]{2,1,0:T(8,128)S(1)} %collective-permute-done.5, f32[64,128]{1,0:T(8,128)S(1)} %near.1, f32[64,128]{1,0:T(8,128)S(1)} %get-tuple-element.19), kind=kLoop, calls=%fused_computation.7 | loop fusion | flops 40960 | bytes 229376 | tf_op jit(solution)/shard_map/add | solution.py:192
  (2 shorter events, 0.0 us)
Async XLA Ops:
  1.1 8.3 %collective-permute-start.1 = (bf16[832,128]{1,0:T(8,128)(2,1)S(1)}, bf16[832,128]{1,0:T(8,128)(2,1)S(1)}, u32[]{:S(2)}, u32[]{:S(2)}) collective-permute-start(bf16[832,128]{1,0:T(8,128)(2,1)S(1)} %pack.1.refs_0_), channel_id=1, source_target_pairs={{0,2},{1,3},{2,0},{3,1},{4,6},{5,7},{6,4},{7,5},{8,10},{9,11},{10,... | collective-permute-start | bytes 638984 | tf_op jit(solution)/shard_map/ppermute | solution.py:159
  4.1 10.1 %collective-permute-start = (bf16[832,128]{1,0:T(8,128)(2,1)S(1)}, bf16[832,128]{1,0:T(8,128)(2,1)S(1)}, u32[]{:S(2)}, u32[]{:S(2)}) collective-permute-start(bf16[832,128]{1,0:T(8,128)(2,1)S(1)} %pack.1.refs_0_), channel_id=1, source_target_pairs={{0,1},{1,0},{2,3},{3,2},{4,5},{5,4},{6,7},{7,6},{8,9},{9,8},{10,11... | collective-permute-start | bytes 638984 | tf_op jit(solution)/shard_map/ppermute | solution.py:159
  4.2 10.1 %collective-permute-start.4 = (bf16[832,128]{1,0:T(8,128)(2,1)S(1)}, bf16[832,128]{1,0:T(8,128)(2,1)S(1)}, u32[]{:S(2)}, u32[]{:S(2)}) collective-permute-start(bf16[832,128]{1,0:T(8,128)(2,1)S(1)} %pack.1.refs_0_), channel_id=1, source_target_pairs={{0,5},{1,4},{2,7},{3,6},{4,9},{5,8},{6,11},{7,10},{8,13},{9,12},{1... | collective-permute-start | bytes 638984 | tf_op jit(solution)/shard_map/ppermute | solution.py:164
  9.4 4.9 %collective-permute-start.2 = (bf16[832,128]{1,0:T(8,128)(2,1)S(1)}, bf16[832,128]{1,0:T(8,128)(2,1)S(1)}, u32[]{:S(2)}, u32[]{:S(2)}) collective-permute-start(bf16[832,128]{1,0:T(8,128)(2,1)S(1)} %collective-permute-done.1.refs_2_), channel_id=1, source_target_pairs={{0,1},{1,0},{2,3},{3,2},{4,5},{5,4},{6,7},{7,6},{8,9},{9,8},{10,11... | collective-permute-start | bytes 638984 | tf_op jit(solution)/shard_map/ppermute | solution.py:159
  9.4 9.8 %collective-permute-start.3 = (bf16[832,128]{1,0:T(8,128)(2,1)S(1)}, bf16[832,128]{1,0:T(8,128)(2,1)S(1)}, u32[]{:S(2)}, u32[]{:S(2)}) collective-permute-start(bf16[832,128]{1,0:T(8,128)(2,1)S(1)} %pack.1.refs_0_), channel_id=1, source_target_pairs={{0,9},{1,8},{2,11},{3,10},{12,5},{13,4},{14,7},{15,6},{16,25},{17,... | collective-permute-start | bytes 638984 | tf_op jit(solution)/shard_map/ppermute | solution.py:164
  19.7 4.5 %collective-permute-start.5 = (f32[2,64,128]{2,1,0:T(8,128)S(1)}, f32[2,64,128]{2,1,0:T(8,128)S(1)}, u32[]{:S(2)}, u32[]{:S(2)}) collective-permute-start(f32[2,64,128]{2,1,0:T(8,128)S(1)} %pad_maximum_fusion), channel_id=1, source_target_pairs={{0,1},{1,0},{2,3},{3,2},{4,5},{5,4},{6,7},{7,6},{8,9},{9,8},{10,11... | collective-permute-start | bytes 196616 | tf_op jit(solution)/shard_map/ppermute | solution.py:159
  19.8 6.5 %collective-permute-start.7 = (f32[64,128]{1,0:T(8,128)S(1)}, f32[64,128]{1,0:T(8,128)S(1)}, u32[]{:S(2)}, u32[]{:S(2)}) collective-permute-start(f32[64,128]{1,0:T(8,128)S(1)} %get-tuple-element.23), channel_id=1, source_target_pairs={{8,1},{9,0},{10,3},{11,2},{4,13},{5,12},{6,15},{7,14},{0,5},{1,4},... | collective-permute-start | bytes 98312 | tf_op jit(solution)/shard_map/ppermute | solution.py:164
  21.7 4.6 %collective-permute-start.6 = (f32[64,128]{1,0:T(8,128)S(1)}, f32[64,128]{1,0:T(8,128)S(1)}, u32[]{:S(2)}, u32[]{:S(2)}) collective-permute-start(f32[64,128]{1,0:T(8,128)S(1)} %get-tuple-element.22), channel_id=1, source_target_pairs={{4,1},{5,0},{6,3},{7,2},{8,5},{9,4},{10,7},{11,6},{12,9},{13,8},{1... | collective-permute-start | bytes 98312 | tf_op jit(solution)/shard_map/ppermute | solution.py:164
  24.2 4.0 %collective-permute-start.8 = (f32[64,128]{1,0:T(8,128)S(1)}, f32[64,128]{1,0:T(8,128)S(1)}, u32[]{:S(2)}, u32[]{:S(2)}) collective-permute-start(f32[64,128]{1,0:T(8,128)S(1)} %fusion), channel_id=1, source_target_pairs={{0,2},{1,3},{2,0},{3,1},{4,6},{5,7},{6,4},{7,5},{8,10},{9,11},{10,... | collective-permute-start | bytes 98312 | tf_op jit(solution)/shard_map/ppermute | solution.py:159
